TPU v7x, 32 devices: a whole 2x2x4 slice. The times are simulated.
32 devices in a mesh: grp: 8 (over y, x, core), col: 4 (over z).
Axes of the slice: x: 2, y: 2, z: 4, core: 2. Of those that a mesh axis runs over, the one named last changes fastest.
Arguments:
- old_tables: bfloat16 [32, 128, 32768], P(('grp', 'col')), may hold values from -3 to 3
- table_rows: int32 [32], replicated, may hold values from 4096 to 32768, as said below
- old_plan: int32 [32], replicated, may hold values from 0 to 31, each once
- new_plan: int32 [32], replicated, may hold values from 0 to 31, each once
- ids: int32 [256, 32, 16], P(('grp', 'col')), may hold values from 0 to 32767, as said below
- bag_len: int32 [256, 32], P(('grp', 'col')), may hold values from 1 to 16
Outputs:
- new_tables: bfloat16 [32, 128, 32768], P('grp', 'col')
- pooled: float32 [256, 32, 128], P(('grp', 'col'))
Inputs may be any that keep to these rules, and one draw needn't show every extreme that they name: table_rows[t] is a multiple of 4096, and some table has exactly 32768 rows. `ids`: every id of table t lies below table_rows[t].
All inputs are finite; a program needn't handle non-finite values.
Results may differ from a plain program's by a relative error of at most 0.001.
Values may be sent and summed in bfloat16 or wider, within the bound.
No kernel may reach another device: no remote copies, remote signals or barrier semaphores. Data moves between devices by JAX's collectives and lax.ppermute only.
A program may use at most 128 MiB of HBM per device.

v0:
```python
import jax
import jax.numpy as jnp
from jax import lax
from jax.sharding import PartitionSpec as P


def invert(permutation):
    entries = permutation.shape[0]
    across = lax.broadcasted_iota(jnp.int32, (entries, entries), 1)
    down = lax.broadcasted_iota(jnp.int32, (entries, entries), 0)
    return jnp.sum(jnp.where(permutation[None, :] == down, across, 0), axis=1)


def pool_rows(table_cols, marked):
    columns = table_cols.shape[0]
    safe_ids = jnp.maximum(marked, 0).reshape(-1)
    weights = (marked >= 0).astype(jnp.float32)
    picked = (
        jnp.take(table_cols, safe_ids, axis=1)
        .reshape(columns, marked.shape[0], marked.shape[1])
        .astype(jnp.float32)
    )
    return jnp.sum(picked * weights[None, :, :], axis=2)


def reorder_blocks(spread, source_rows):
    count = spread.shape[0]
    across = lax.broadcasted_iota(jnp.int32, (count, count), 1)
    selector = (source_rows[:, None] == across).astype(spread.dtype)
    flat = spread.reshape(count, -1)
    picked = jnp.dot(selector, flat, preferred_element_type=jnp.float32).astype(spread.dtype)
    return picked.reshape(spread.shape)


def body(old_tables, table_rows, old_plan, new_plan, ids, bag_len):
    group_count = lax.axis_size("grp")
    col_count = lax.axis_size("col")
    device_count = group_count * col_count
    full_width = old_tables.shape[1]
    table_len = old_tables.shape[2]
    row_block = table_len // device_count
    narrow = full_width // col_count
    per_group = new_plan.shape[0] // group_count
    bag_size = ids.shape[2]
    own_slot = lax.axis_index("grp") * col_count + lax.axis_index("col")
    own_table = old_plan[own_slot]
    row_limit = table_rows[own_table]
    row_iota = lax.broadcasted_iota(jnp.int32, (1, table_len), 1)
    owned_table = old_tables[0] * (row_iota < row_limit).astype(old_tables.dtype)
    spread = lax.all_to_all(
        owned_table.reshape(full_width, device_count, row_block),
        ("grp", "col"),
        split_axis=1,
        concat_axis=0,
        tiled=True,
    )
    spread = spread.reshape(device_count * col_count, narrow, row_block)
    old_inverse = invert(old_plan)
    source_slot = old_inverse[new_plan].reshape(group_count, 1, per_group)
    source_rows = (
        source_slot * col_count + lax.broadcasted_iota(jnp.int32, (1, col_count, 1), 1)
    ).reshape(-1)
    blocks = reorder_blocks(spread, source_rows)
    direct = lax.all_to_all(
        blocks.reshape(device_count, per_group, narrow, row_block),
        ("grp", "col"),
        split_axis=0,
        concat_axis=3,
        tiled=True,
    )
    new_local = direct.reshape(per_group, narrow, table_len)
    bag_iota = lax.broadcasted_iota(jnp.int32, (1, 1, bag_size), 2)
    marked = jnp.where(bag_iota < bag_len[:, :, None], ids, -1)
    by_slot = jnp.take(marked, old_plan, axis=1)
    own_ids = lax.all_to_all(
        by_slot, ("grp", "col"), split_axis=1, concat_axis=0, tiled=True
    ).reshape(-1, bag_size)
    partial_value = pool_rows(owned_table, own_ids)
    returned = lax.all_to_all(
        partial_value.reshape(1, full_width, -1),
        ("grp", "col"),
        split_axis=2,
        concat_axis=0,
        tiled=True,
    )
    by_table = jnp.take(returned, old_inverse, axis=0)
    pooled = jnp.transpose(by_table, (2, 0, 1))
    return (new_local, pooled)


def solution(mesh):
    return jax.shard_map(
        body,
        mesh=mesh,
        in_specs=(
            P(("grp", "col"), None, None),
            P(),
            P(),
            P(),
            P(("grp", "col"), None, None),
            P(("grp", "col"), None),
        ),
        out_specs=(P("grp", "col", None), P(("grp", "col"), None, None)),
        check_vma=False,
    )
```

profile of v0, /device:TPU:9, one launch (start us, length us, event | category | flops | bytes accessed | tf_op | source)
XLA Modules:
  0.0 492.5 jit_solution(5518799861332294195)
XLA Ops:
  0.6 0.7 compare_select_fusion.1
  1.3 0.7 compare_and_fusion
  2.0 0.9 copy.25
  2.9 0.8 copy.24
  3.7 0.1 fusion.1
  3.8 0.6 gather_fusion.1
  4.4 0.1 fusion.5
  4.5 0.7 reshape.168
  5.2 6.3 %all-to-all-start.2 = ((s32[32,1,128]{2,1,0:T(1,128)}), s32[32,1,128]{2,1,0:T(1,128)S(1)}, u32[]{:S(2)}, u32[]{:S(2)}) async-start(s32[32,1,128]{2,1,0:T(1,128)} %reshape.168), calls=%async_computation.2 | async-start | bytes 32768 | tf_op jit(solution)/shard_map/all_to_all | solution.py:75
  11.5 1.2 dynamic_slice.6
  14.7 1.3 dynamic_slice.7
  16.0 0.7 fusion
  16.7 12.4 %copy.28 = bf16[16,8,32,1024]{3,2,1,0:T(8,128)(2,1)} copy(bf16[16,8,32,1024]{3,1,2,0:T(8,128)(2,1)} %bitcast.70) | data formatting | bytes 16777216
  29.1 16.0 %copy_multiply_fusion = bf16[128,32,1024]{2,0,1:T(8,128)(2,1)} fusion(bf16[128,32,1024]{2,1,0:T(8,128)(2,1)} %bitcast.72, bf16[32,1024]{1,0:T(8,128)(2,1)S(1)} %fusion), kind=kLoop, calls=%fused_computation.6 | loop fusion | flops 4194304 | bytes 16842752 | tf_op jit(solution)/shard_map/mul | solution.py:49
  45.1 0.0 all-to-all-done.2
  45.1 5.9 %all-to-all-start = ((bf16[128,32,1024]{2,0,1:T(8,128)(2,1)}), bf16[128,32,1024]{2,0,1:T(8,128)(2,1)}, u32[]{:S(2)}, u32[]{:S(2)}) async-start(bf16[128,32,1024]{2,0,1:T(8,128)(2,1)} %copy_multiply_fusion), calls=%async_computation | async-start | bytes 16777216 | tf_op jit(solution)/shard_map/all_to_all | solution.py:50
  51.0 0.0 copy-start
  51.0 0.0 copy-start.1
  51.0 11.9 %copy.26 = bf16[1,128,32768]{1,2,0:T(8,128)(2,1)} copy(bf16[1,128,32768]{2,1,0:T(8,128)(2,1)} %param.6) | data formatting | bytes 16777216 | tf_op args[0]
  62.9 0.0 copy-done
  62.9 0.0 copy-done.1
  62.9 0.1 select_reduce_fusion
  63.0 0.7 gather_fusion
  63.7 0.1 mul.40
  63.8 0.1 add.73
  64.0 0.7 fusion.2
  64.6 8.6 %bitcast_multiply_fusion = bf16[128,32768]{0,1:T(8,128)(2,1)} fusion(bf16[1,128,32768]{1,2,0:T(8,128)(2,1)} %copy.26, bf16[32768]{0:T(1024)(128)(2,1)S(1)} %fusion.2), kind=kLoop, calls=%fused_computation.5 | loop fusion | flops 4194304 | bytes 16842752 | tf_op jit(solution)/shard_map/mul | solution.py:49
  73.2 0.5 broadcast.144
  73.7 0.7 reduce
  74.4 0.1 reshape.169
  74.5 0.1 reshape.151
  74.6 15.5 %gather_fusion.2 = bf16[4096,128]{1,0:T(8,128)(2,1)S(1)} fusion(bf16[128,32768]{0,1:T(8,128)(2,1)} %bitcast_multiply_fusion, s32[4096]{0:T(1024)S(1)} %broadcast_clamp_fusion), kind=kCustom, calls=%fused_computation.2 | custom fusion | bytes 2113536 | tf_op jit(solution)/shard_map/jit(_take)/gather | solution.py:19
  90.1 2.2 multiply_reduce_fusion
  92.3 144.8 %all-to-all-done = bf16[128,32,1024]{2,0,1:T(8,128)(2,1)} async-done(((bf16[128,32,1024]{2,0,1:T(8,128)(2,1)}), bf16[128,32,1024]{2,0,1:T(8,128)(2,1)}, u32[]{:S(2)}, u32[]{:S(2)}) %all-to-all-start) | async-done | bytes 8388640 | tf_op jit(solution)/shard_map/all_to_all | solution.py:50
  237.1 3.7 all-to-all-start.3
  240.8 13.4 %reshape_reshape.6 = bf16[128,32768]{1,0:T(8,128)(2,1)} reshape(bf16[32,128,1,1024]{3,1,0,2:T(8,128)(2,1)} %bitcast.3) | data formatting | bytes 16777216 | tf_op jit(solution)/shard_map/reshape;reshape | solution.py:30
  254.2 9.0 %convolution_convert_fusion = bf16[128,32768]{1,0:T(8,128)(2,1)} fusion(bf16[128,32768]{1,0:T(8,128)(2,1)} %reshape_reshape.6, s32[128]{0:T(128)S(1)} %add.73), kind=kOutput, calls=%fused_computation.4 | convolution fusion | flops 1077952512 | bytes 16777728 | tf_op jit(solution)/shard_map/dot_general | solution.py:31
  263.2 12.4 %copy.29 = bf16[16,8,32,1024]{3,2,1,0:T(8,128)(2,1)} copy(bf16[16,8,32,1024]{3,1,2,0:T(8,128)(2,1)} %bitcast.69) | data formatting | bytes 16777216
  275.6 0.0 all-to-all-done.3
  275.6 5.9 %all-to-all-start.1 = ((bf16[32,4,32,1024]{3,2,1,0:T(8,128)(2,1)}), bf16[32,4,32,1024]{3,2,1,0:T(8,128)(2,1)}, u32[]{:S(2)}, u32[]{:S(2)}) async-start(bf16[32,4,32,1024]{3,2,1,0:T(8,128)(2,1)} %bitcast.71), calls=%async_computation.1 | async-start | bytes 16777216 | tf_op jit(solution)/shard_map/all_to_all | solution.py:64
  281.6 0.6 gather_fusion.3
  282.2 0.1 select_bitcast_fusion.1
  282.3 0.7 copy.27
  282.9 184.7 %all-to-all-done.1 = bf16[32,4,32,1024]{3,2,1,0:T(8,128)(2,1)} async-done(((bf16[32,4,32,1024]{3,2,1,0:T(8,128)(2,1)}), bf16[32,4,32,1024]{3,2,1,0:T(8,128)(2,1)}, u32[]{:S(2)}, u32[]{:S(2)}) %all-to-all-start.1) | async-done | bytes 8388640 | tf_op jit(solution)/shard_map/all_to_all | solution.py:64
  467.7 11.4 %copy.23 = bf16[1,4,32,32,1024]{4,3,2,1,0:T(8,128)(2,1)} copy(bf16[1,4,32,32,1024]{4,2,1,3,0:T(8,128)(2,1)} %bitcast.5) | data formatting | bytes 16777216 | tf_op jit(solution)/shard_map/all_to_all | solution.py:64
  479.1 13.4 %reshape.129 = bf16[4,32,32768]{2,1,0:T(8,128)(2,1)} reshape(bf16[1,4,32,32,1024]{4,3,2,1,0:T(8,128)(2,1)} %copy.23) | data formatting | bytes 16777216 | tf_op jit(solution)/shard_map/reshape | solution.py:71
  (11 shorter events, 0.1 us)
Async XLA Ops:
  5.2 39.9 %all-to-all-start.2 = ((s32[32,1,128]{2,1,0:T(1,128)}), s32[32,1,128]{2,1,0:T(1,128)S(1)}, u32[]{:S(2)}, u32[]{:S(2)}) async-start(s32[32,1,128]{2,1,0:T(1,128)} %reshape.168), calls=%async_computation.2 | async-start | bytes 32768 | tf_op jit(solution)/shard_map/all_to_all | solution.py:75
  45.1 192.0 %all-to-all-start = ((bf16[128,32,1024]{2,0,1:T(8,128)(2,1)}), bf16[128,32,1024]{2,0,1:T(8,128)(2,1)}, u32[]{:S(2)}, u32[]{:S(2)}) async-start(bf16[128,32,1024]{2,0,1:T(8,128)(2,1)} %copy_multiply_fusion), calls=%async_computation | async-start | bytes 16777216 | tf_op jit(solution)/shard_map/all_to_all | solution.py:50
  51.0 11.9 %copy-start = (s32[32]{0:T(128)S(1)}, s32[32]{0:T(128)}, u32[]{:S(2)}) copy-start(s32[32]{0:T(128)} %param.9) | copy-start | bytes 388
  51.0 11.9 %copy-start.1 = (s32[32]{0:T(128)S(1)}, s32[32]{0:T(128)}, u32[]{:S(2)}) copy-start(s32[32]{0:T(128)} %param.8) | copy-start | bytes 388
  237.1 38.5 %all-to-all-start.3 = ((f32[1,128,256]{1,0,2:T(1,128)}), f32[1,128,256]{1,0,2:T(1,128)S(1)}, u32[]{:S(2)}, u32[]{:S(2)}) async-start(f32[1,128,256]{1,0,2:T(1,128)} %bitcast.18), calls=%async_computation.3 | async-start | bytes 262144 | tf_op jit(solution)/shard_map/all_to_all | solution.py:79
  275.6 192.0 %all-to-all-start.1 = ((bf16[32,4,32,1024]{3,2,1,0:T(8,128)(2,1)}), bf16[32,4,32,1024]{3,2,1,0:T(8,128)(2,1)}, u32[]{:S(2)}, u32[]{:S(2)}) async-start(bf16[32,4,32,1024]{3,2,1,0:T(8,128)(2,1)} %bitcast.71), calls=%async_computation.1 | async-start | bytes 16777216 | tf_op jit(solution)/shard_map/all_to_all | solution.py:64
where the time goes:
time: 494 us; the launch traced here: 492 us
  waiting for transfers between devices  329 us (67%)
  local copies, waits for them, and re-layouts  98.9 us (20%)
  other arithmetic  30.6 us (6%)
  starting transfers between devices  21.8 us (4%)
  matrix products  8.98 us (2%)
    all_to_all x1, waiting for transfers between devices, body(): lax.all_to_all(blocks.reshape(device_count, per_group, narrow, row_block)...  185 us
    all_to_all x1, waiting for transfers between devices, body(): lax.all_to_all(owned_table.reshape(full_width, device_count, row_block),...  145 us
    unnamed x12, local copies, waits for them, and re-layouts  39.9 us
    mul x2, other arithmetic, body(): old_tables[0] * (row_iota < row_limit).astype(old_tables.dtype)  24.6 us
    gather x1, local copies, waits for them, and re-layouts, pool_rows(): jnp.take(table_cols, safe_ids, axis=1)  15.5 us
    another operation x1, local copies, waits for them, and re-layouts, reorder_blocks(): flat = spread.reshape(count, -1)  13.4 us
    reshape x1, local copies, waits for them, and re-layouts, body(): new_local = direct.reshape(per_group, narrow, table_len)  13.4 us
    all_to_all x1, local copies, waits for them, and re-layouts, body(): lax.all_to_all(blocks.reshape(device_count, per_group, narrow, row_block)...  11.4 us
  transfers between devices with their start and end apart: 4, of which 2 were waited for; matrix products, arithmetic and copies ran while one was open for 22% of the time, Pallas kernels for 0%

commit v1 on v0

v1 whole, which is shorter than its diff:
```python
import jax
import jax.numpy as jnp
from jax import lax
from jax.experimental import pallas as pl
from jax.experimental.pallas import tpu as pltpu
from jax.sharding import PartitionSpec as P


CHUNKS = 4


def invert(permutation):
    entries = permutation.shape[0]
    across = lax.broadcasted_iota(jnp.int32, (entries, entries), 1)
    down = lax.broadcasted_iota(jnp.int32, (entries, entries), 0)
    return jnp.sum(jnp.where(permutation[None, :] == down, across, 0), axis=1)


def pool_rows(table_cols, marked):
    columns = table_cols.shape[0]
    safe_ids = jnp.maximum(marked, 0).reshape(-1)
    weights = (marked >= 0).astype(jnp.float32)
    picked = (
        jnp.take(table_cols, safe_ids, axis=1)
        .reshape(columns, marked.shape[0], marked.shape[1])
        .astype(jnp.float32)
    )
    return jnp.sum(picked * weights[None, :, :], axis=2)


def split_chunk(table, slot, plan, used_rows, chunk, group_count, col_count):
    full_width, table_len = table.shape
    height = full_width // col_count // CHUNKS
    block = table_len // group_count

    def kernel(slot_ref, plan_ref, used_ref, x_ref, o_ref):
        limit = used_ref[plan_ref[slot_ref[0]]]
        for g in range(group_count):
            rows = lax.broadcasted_iota(jnp.int32, (height, block), 1) + g * block
            piece = x_ref[:, g * block:(g + 1) * block]
            o_ref[g, 0] = jnp.where(rows < limit, piece, jnp.zeros_like(piece))

    return pl.pallas_call(
        kernel,
        grid_spec=pltpu.PrefetchScalarGridSpec(
            num_scalar_prefetch=3,
            grid=(col_count,),
            in_specs=[pl.BlockSpec((height, table_len), lambda c, *_: (c * CHUNKS + chunk, 0))],
            out_specs=pl.BlockSpec((group_count, 1, height, block), lambda c, *_: (0, c, 0, 0)),
        ),
        out_shape=jax.ShapeDtypeStruct((group_count, col_count, height, block), table.dtype),
    )(slot, plan, used_rows, table)


def peer(own, shift, group_count):
    if group_count & (group_count - 1) == 0:
        return own ^ shift
    return (own + shift) % group_count


def peer_pairs(shift, group_count):
    return [(own, peer(own, shift, group_count)) for own in range(group_count)]


def pick_blocks(blocks, source_slot, group_count, per_group):
    _, height, block = blocks.shape

    def kernel(slot_ref, *refs):
        for k in range(group_count):
            refs[group_count + k][...] = refs[k][...]

    def source(k):
        return pl.BlockSpec((1, height, block), lambda p, slots: (slots[k * per_group + p], 0, 0))

    return pl.pallas_call(
        kernel,
        grid_spec=pltpu.PrefetchScalarGridSpec(
            num_scalar_prefetch=1,
            grid=(per_group,),
            in_specs=[source(k) for k in range(group_count)],
            out_specs=[pl.BlockSpec((1, height, block), lambda p, _: (p, 0, 0))] * group_count,
        ),
        out_shape=[jax.ShapeDtypeStruct((per_group, height, block), blocks.dtype)] * group_count,
    )(source_slot, *([blocks] * group_count))


def join_chunk(landed, places, out, chunk):
    group_count = len(landed)
    per_group, height, block = landed[0].shape

    def kernel(place_ref, *refs):
        o_ref = refs[-1]
        for k in range(group_count):
            o_ref[0, :, pl.ds(pl.multiple_of(place_ref[k] * block, block), block)] = refs[k][0]

    shape = jax.ShapeDtypeStruct((per_group, height * CHUNKS, group_count * block), landed[0].dtype)
    first = out is None
    return pl.pallas_call(
        kernel,
        grid_spec=pltpu.PrefetchScalarGridSpec(
            num_scalar_prefetch=1,
            grid=(per_group,),
            in_specs=[pl.BlockSpec((1, height, block), lambda p, _: (p, 0, 0))] * group_count
            + ([] if first else [pl.BlockSpec(memory_space=pl.ANY)]),
            out_specs=pl.BlockSpec((1, height, group_count * block), lambda p, _: (p, chunk, 0)),
        ),
        out_shape=shape,
        input_output_aliases={} if first else {group_count + 1: 0},
    )(places, *landed, *(() if first else (out,)))


def move(old_tables, table_rows, old_plan, new_plan, ids, bag_len):
    group_count = lax.axis_size("grp")
    col_count = lax.axis_size("col")
    device_count = group_count * col_count
    full_width = old_tables.shape[1]
    table_len = old_tables.shape[2]
    row_block = table_len // group_count
    height = full_width // col_count // CHUNKS
    per_group = new_plan.shape[0] // group_count
    bag_size = ids.shape[2]
    own_slot = lax.axis_index("grp") * col_count + lax.axis_index("col")
    slot = own_slot.astype(jnp.int32).reshape(1)
    table = old_tables[0]

    pieces = []
    for k in range(CHUNKS):
        pieces.append(split_chunk(table, slot, old_plan, table_rows, k, group_count, col_count))
    bag_iota = lax.broadcasted_iota(jnp.int32, (1, 1, bag_size), 2)
    marked = jnp.where(bag_iota < bag_len[:, :, None], ids, -1)
    by_slot = jnp.take(marked, old_plan, axis=1)
    own_ids = lax.all_to_all(
        by_slot, ("grp", "col"), split_axis=1, concat_axis=0, tiled=True
    ).reshape(-1, bag_size)
    partial_value = pool_rows(table, own_ids)
    pieces[2], partial_value = lax.optimization_barrier((pieces[2], partial_value))
    old_inverse = invert(old_plan)
    source_slot = old_inverse[new_plan]
    own_group = lax.axis_index("grp").astype(jnp.int32)
    places = peer(own_group, jnp.arange(group_count, dtype=jnp.int32), group_count)
    sources = places
    by_peer = source_slot.reshape(group_count, per_group)[sources].reshape(-1)
    new_local = None
    for k in range(CHUNKS):
        got = lax.all_to_all(
            pieces[k].reshape(device_count, height, row_block),
            ("grp", "col"),
            split_axis=0,
            concat_axis=0,
            tiled=True,
        )
        send = pick_blocks(got, by_peer, group_count, per_group)
        landed = [send[0]] + [
            lax.ppermute(send[shift], "grp", peer_pairs(shift, group_count))
            for shift in range(1, group_count)
        ]
        new_local = join_chunk(landed, places, new_local, k)

    returned = lax.all_to_all(
        partial_value.reshape(1, full_width, -1),
        ("grp", "col"),
        split_axis=2,
        concat_axis=0,
        tiled=True,
    )
    by_table = jnp.take(returned, old_inverse, axis=0)
    pooled = jnp.transpose(by_table, (2, 0, 1))
    return (new_local, pooled)


def solution(mesh):
    return jax.shard_map(
        move,
        mesh=mesh,
        in_specs=(
            P(("grp", "col"), None, None),
            P(),
            P(),
            P(),
            P(("grp", "col"), None, None),
            P(("grp", "col"), None),
        ),
        out_specs=(P("grp", "col", None), P(("grp", "col"), None, None)),
        check_vma=False,
    )
```

time: 494 us -> 313 us (0.63)
  waiting for transfers between devices: 329 us -> 150 us
  local copies, waits for them, and re-layouts: 98.9 us -> 40.2 us
  Pallas kernels: 0 us -> 54.2 us
  starting transfers between devices: 21.8 us -> 57.4 us
  other arithmetic: 30.6 us -> 5.25 us
  matrix products: 8.98 us -> 0 us
    all_to_all x4 -> x6, waiting for transfers between devices: 329 us -> 99 us  [the longest x4 98 us: move(): lax.all_to_all(pieces[k].reshape(device_count, height, row_block), ('grp'...]
    pallas_call x0 -> x12, Pallas kernels: none -> 54.2 us  [the longest x4 18.6 us: split_chunk(): pl.pallas_call(kernel, grid_spec=pltpu.PrefetchScalarGridSpec(num_scalar_...]
    ppermute x0 -> x28, waiting for transfers between devices: none -> 50.6 us  [move(): lax.ppermute(send[shift], 'grp', peer_pairs(shift, group_count))]
    unnamed x12 -> x69, local copies, waits for them, and re-layouts: 39.9 us -> 9.02 us
    ppermute x0 -> x28, starting transfers between devices: none -> 25.3 us  [move(): lax.ppermute(send[shift], 'grp', peer_pairs(shift, group_count))]
    mul x3 -> x0, other arithmetic: 24.6 us -> none  [the longest x2 24.6 us: body(): old_tables[0] * (row_iota < row_limit).astype(old_tables.dtype)]
    another operation x1 -> x0, local copies, waits for them, and re-layouts: 13.4 us -> none  [reorder_blocks(): flat = spread.reshape(count, -1)]
    reshape x1 -> x2, local copies, waits for them, and re-layouts: 13.4 us -> 0.73 us  [move(): by_peer = source_slot.reshape(group_count, per_group)[sources].reshape(-1)]
  transfers between devices with their start and end apart: 4 -> 34, of which waited for: 2 -> 13; matrix products, arithmetic and copies ran while one was open for 22% -> 11% of each run, Pallas kernels for 0% -> 16%
where the time goes in v1:
time: 313 us; the launch traced here: 308 us
  waiting for transfers between devices  150 us (48%)
  starting transfers between devices  57.4 us (18%)
  Pallas kernels  54.2 us (17%)
  local copies, waits for them, and re-layouts  40.2 us (13%)
  other arithmetic  5.25 us (2%)
    all_to_all x4, waiting for transfers between devices, move(): lax.all_to_all(pieces[k].reshape(device_count, height, row_block), ('grp'...  98 us
    ppermute x28, waiting for transfers between devices, move(): lax.ppermute(send[shift], 'grp', peer_pairs(shift, group_count))  50.6 us
    ppermute x28, starting transfers between devices, move(): lax.ppermute(send[shift], 'grp', peer_pairs(shift, group_count))  25.3 us
    pallas_call x4, Pallas kernels, split_chunk(): pl.pallas_call(kernel, grid_spec=pltpu.PrefetchScalarGridSpec(num_scalar_...  18.6 us
    pallas_call x4, Pallas kernels, pick_blocks(): pl.pallas_call(kernel, grid_spec=pltpu.PrefetchScalarGridSpec(num_scalar_...  17.9 us
    pallas_call x4, Pallas kernels, join_chunk(): pl.pallas_call(kernel, grid_spec=pltpu.PrefetchScalarGridSpec(num_scalar_...  17.7 us
    all_to_all x4, starting transfers between devices, move(): lax.all_to_all(pieces[k].reshape(device_count, height, row_block), ('grp'...  16.3 us
    gather x1, local copies, waits for them, and re-layouts, pool_rows(): jnp.take(table_cols, safe_ids, axis=1)  15.5 us
  transfers between devices with their start and end apart: 34, of which 13 were waited for; matrix products, arithmetic and copies ran while one was open for 11% of the time, Pallas kernels for 16%

profile of v1, /device:TPU:9, one launch (start us, length us, event | category | flops | bytes accessed | tf_op | source)
XLA Modules:
  0.0 307.8 jit_solution(7937715703538909536)
XLA Ops:
  5.2 6.3 %all-to-all-start.1 = ((s32[32,1,128]{2,1,0:T(1,128)}), s32[32,1,128]{2,1,0:T(1,128)S(1)}, u32[]{:S(2)}, u32[]{:S(2)}) async-start(s32[32,1,128]{2,1,0:T(1,128)} %reshape.175), calls=%async_computation.1 | async-start | bytes 32768 | tf_op jit(solution)/shard_map/all_to_all | solution.py:132
  11.5 4.7 %shard_map.83 = bf16[8,4,8,4096]{3,2,1,0:T(8,128)(2,1)} custom-call(s32[1]{0:T(128)} %bitcast.1.slot_ref, s32[32]{0:T(128)} %plan_ref.7, s32[32]{0:T(128)} %used_ref.7, bf16[128,32768]{1,0:T(8,128)(2,1)} %bitcast.53), custom_call_target="tpu_custom_call" | custom-call | tf_op jit(solution)/shard_map/pallas_call | solution.py:43
  16.2 0.9 all-to-all-done.1
  17.1 4.9 %all-to-all-start.4 = ((bf16[32,8,4096]{2,1,0:T(8,128)(2,1)}), bf16[32,8,4096]{2,1,0:T(8,128)(2,1)S(1)}, u32[]{:S(2)}, u32[]{:S(2)}) async-start(bf16[32,8,4096]{2,1,0:T(8,128)(2,1)} %bitcast.61), calls=%async_computation.4 | async-start | bytes 4194304 | tf_op jit(solution)/shard_map/all_to_all | solution.py:145
  22.0 4.6 %shard_map.81 = bf16[8,4,8,4096]{3,2,1,0:T(8,128)(2,1)} custom-call(s32[1]{0:T(128)} %bitcast.1.slot_ref, s32[32]{0:T(128)} %plan_ref.7, s32[32]{0:T(128)} %used_ref.7, bf16[128,32768]{1,0:T(8,128)(2,1)} %bitcast.54), custom_call_target="tpu_custom_call" | custom-call | tf_op jit(solution)/shard_map/pallas_call | solution.py:43
  26.6 43.1 %all-to-all-done.4.refs_0_.refs_1_.refs_2_.refs_3_.refs_4_.refs_5_.refs_6_.refs_7_ = bf16[32,8,4096]{2,1,0:T(8,128)(2,1)S(1)} async-done(((bf16[32,8,4096]{2,1,0:T(8,128)(2,1)}), bf16[32,8,4096]{2,1,0:T(8,128)(2,1)S(1)}, u32[]{:S(2)}, u32[]{:S(2)}) %all-to-all-start.4) | async-done | bytes 2097184 | tf_op jit(solution)/shard_map/all_to_all | solution.py:145
  69.7 1.4 copy-done.2
  71.1 3.8 %all-to-all-start.3 = ((bf16[32,8,4096]{2,1,0:T(8,128)(2,1)}), bf16[32,8,4096]{2,1,0:T(8,128)(2,1)S(1)}, u32[]{:S(2)}, u32[]{:S(2)}) async-start(bf16[32,8,4096]{2,1,0:T(8,128)(2,1)} %bitcast.62), calls=%async_computation.3 | async-start | bytes 4194304 | tf_op jit(solution)/shard_map/all_to_all | solution.py:145
  74.9 4.7 %shard_map.77 = bf16[8,4,8,4096]{3,2,1,0:T(8,128)(2,1)} custom-call(s32[1]{0:T(128)} %bitcast.1.slot_ref, s32[32]{0:T(128)} %plan_ref.7, s32[32]{0:T(128)} %used_ref.7, bf16[128,32768]{1,0:T(8,128)(2,1)} %bitcast.55), custom_call_target="tpu_custom_call" | custom-call | tf_op jit(solution)/shard_map/pallas_call | solution.py:43
  79.5 43.0 %all-to-all-done.3.refs_0_.refs_1_.refs_2_.refs_3_.refs_4_.refs_5_.refs_6_.refs_7_ = bf16[32,8,4096]{2,1,0:T(8,128)(2,1)S(1)} async-done(((bf16[32,8,4096]{2,1,0:T(8,128)(2,1)}), bf16[32,8,4096]{2,1,0:T(8,128)(2,1)S(1)}, u32[]{:S(2)}, u32[]{:S(2)}) %all-to-all-start.3) | async-done | bytes 2097184 | tf_op jit(solution)/shard_map/all_to_all | solution.py:145
  122.6 1.4 copy-done.1
  123.9 3.8 %all-to-all-start = ((bf16[32,8,4096]{2,1,0:T(8,128)(2,1)}), bf16[32,8,4096]{2,1,0:T(8,128)(2,1)S(1)}, u32[]{:S(2)}, u32[]{:S(2)}) async-start(bf16[32,8,4096]{2,1,0:T(8,128)(2,1)} %bitcast.60), calls=%async_computation | async-start | bytes 4194304 | tf_op jit(solution)/shard_map/all_to_all | solution.py:145
  127.7 4.6 %shard_map.79 = bf16[8,4,8,4096]{3,2,1,0:T(8,128)(2,1)} custom-call(s32[1]{0:T(128)} %bitcast.1.slot_ref, s32[32]{0:T(128)} %plan_ref.7, s32[32]{0:T(128)} %used_ref.7, bf16[128,32768]{1,0:T(8,128)(2,1)} %bitcast.56), custom_call_target="tpu_custom_call" | custom-call | tf_op jit(solution)/shard_map/pallas_call | solution.py:43
  132.4 11.9 %copy.22 = bf16[128,32768]{0,1:T(8,128)(2,1)} copy(bf16[128,32768]{1,0:T(8,128)(2,1)} %bitcast.57) | data formatting | bytes 16777216 | tf_op jit(solution)/shard_map/squeeze | solution.py:124
  145.7 15.5 %gather_fusion.3 = bf16[4096,128]{1,0:T(8,128)(2,1)S(1)} fusion(bf16[128,32768]{0,1:T(8,128)(2,1)} %copy.22, s32[4096]{0:T(1024)S(1)} %broadcast_clamp_fusion), kind=kCustom, calls=%fused_computation.3 | custom fusion | bytes 2113536 | tf_op jit(solution)/shard_map/jit(_take)/gather | solution.py:24
  161.3 2.2 multiply_reduce_fusion
  163.5 11.9 %all-to-all-done.refs_0_.refs_1_.refs_2_.refs_3_.refs_4_.refs_5_.refs_6_.refs_7_ = bf16[32,8,4096]{2,1,0:T(8,128)(2,1)S(1)} async-done(((bf16[32,8,4096]{2,1,0:T(8,128)(2,1)}), bf16[32,8,4096]{2,1,0:T(8,128)(2,1)S(1)}, u32[]{:S(2)}, u32[]{:S(2)}) %all-to-all-start) | async-done | bytes 2097184 | tf_op jit(solution)/shard_map/all_to_all | solution.py:145
  175.4 1.3 copy-done
  176.7 3.8 %all-to-all-start.2 = ((bf16[32,8,4096]{2,1,0:T(8,128)(2,1)}), bf16[32,8,4096]{2,1,0:T(8,128)(2,1)}, u32[]{:S(2)}, u32[]{:S(2)}) async-start(bf16[32,8,4096]{2,1,0:T(8,128)(2,1)} %bitcast.59), calls=%async_computation.2 | async-start | bytes 4194304 | tf_op jit(solution)/shard_map/all_to_all | solution.py:145
  182.8 4.5 %shard_map.84 = (bf16[4,8,4096]{2,1,0:T(8,128)(2,1)}, bf16[4,8,4096]{2,1,0:T(8,128)(2,1)}, bf16[4,8,4096]{2,1,0:T(8,128)(2,1)}, bf16[4,8,4096]{2,1,0:T(8,128)(2,...) custom-call(s32[32]{0:T(128)} %reshape.123.slot_ref, ...), custom_call_target="tpu_custom_call" | custom-call | tf_op jit(solution)/shard_map/pallas_call | solution.py:75
  188.9 1.0 collective-permute-start.23
  190.6 1.0 collective-permute-start.25
  191.6 4.5 %shard_map.82 = (bf16[4,8,4096]{2,1,0:T(8,128)(2,1)}, bf16[4,8,4096]{2,1,0:T(8,128)(2,1)}, bf16[4,8,4096]{2,1,0:T(8,128)(2,1)}, bf16[4,8,4096]{2,1,0:T(8,128)(2,...) custom-call(s32[32]{0:T(128)} %reshape.123.slot_ref, ...), custom_call_target="tpu_custom_call" | custom-call | tf_op jit(solution)/shard_map/pallas_call | solution.py:75
  196.1 1.7 collective-permute-start.26
  197.8 3.7 %collective-permute-done.22.refs_2_ = bf16[4,8,4096]{2,1,0:T(8,128)(2,1)S(1)} collective-permute-done((bf16[4,8,4096]{2,1,0:T(8,128)(2,1)}, bf16[4,8,4096]{2,1,0:T(8,128)(2,1)S(1)}, u32[]{:S(2)}, u32[]{:S(2)}) %collective-permute-start.22) | collective-permute-done | bytes 262176 | tf_op jit(solution)/shard_map/ppermute | solution.py:154
  201.5 2.5 collective-permute-start.27
  204.1 9.8 %collective-permute-done.23.refs_3_ = bf16[4,8,4096]{2,1,0:T(8,128)(2,1)S(1)} collective-permute-done((bf16[4,8,4096]{2,1,0:T(8,128)(2,1)}, bf16[4,8,4096]{2,1,0:T(8,128)(2,1)S(1)}, u32[]{:S(2)}, u32[]{:S(2)}) %collective-permute-start.23) | collective-permute-done | bytes 262176 | tf_op jit(solution)/shard_map/ppermute | solution.py:154
  214.6 2.8 collective-permute-done.25.refs_5_
  217.6 4.2 %collective-permute-done.26.refs_6_ = bf16[4,8,4096]{2,1,0:T(8,128)(2,1)S(1)} collective-permute-done((bf16[4,8,4096]{2,1,0:T(8,128)(2,1)S(1)}, bf16[4,8,4096]{2,1,0:T(8,128)(2,1)S(1)}, u32[]{:S(2)}, u32[]{:S(2)}) %collective-permute-start.26) | collective-permute-done | bytes 262176 | tf_op jit(solution)/shard_map/ppermute | solution.py:154
  222.3 8.1 %collective-permute-done.27.refs_7_ = bf16[4,8,4096]{2,1,0:T(8,128)(2,1)S(1)} collective-permute-done((bf16[4,8,4096]{2,1,0:T(8,128)(2,1)S(1)}, bf16[4,8,4096]{2,1,0:T(8,128)(2,1)S(1)}, u32[]{:S(2)}, u32[]{:S(2)}) %collective-permute-start.27) | collective-permute-done | bytes 262176 | tf_op jit(solution)/shard_map/ppermute | solution.py:154
  232.0 4.5 %shard_map.78 = (bf16[4,8,4096]{2,1,0:T(8,128)(2,1)}, bf16[4,8,4096]{2,1,0:T(8,128)(2,1)}, bf16[4,8,4096]{2,1,0:T(8,128)(2,1)}, bf16[4,8,4096]{2,1,0:T(8,128)(2,...) custom-call(s32[32]{0:T(128)} %reshape.123.slot_ref, ...), custom_call_target="tpu_custom_call" | custom-call | tf_op jit(solution)/shard_map/pallas_call | solution.py:75
  236.5 4.5 %shard_map.80 = (bf16[4,8,4096]{2,1,0:T(8,128)(2,1)}, bf16[4,8,4096]{2,1,0:T(8,128)(2,1)}, bf16[4,8,4096]{2,1,0:T(8,128)(2,1)}, bf16[4,8,4096]{2,1,0:T(8,128)(2,...) custom-call(s32[32]{0:T(128)} %reshape.123.slot_ref, ...), custom_call_target="tpu_custom_call" | custom-call | tf_op jit(solution)/shard_map/pallas_call | solution.py:75
  241.0 1.9 collective-permute-start.20
  244.0 1.1 collective-permute-start.10
  245.1 1.3 collective-permute-done.19.refs_6_
  246.3 1.9 collective-permute-start.11
  248.2 9.4 %all-to-all-start.5 = ((f32[1,128,256]{1,0,2:T(1,128)}), f32[1,128,256]{1,0,2:T(1,128)S(1)}, u32[]{:S(2)}, u32[]{:S(2)}) async-start(f32[1,128,256]{1,0,2:T(1,128)} %bitcast.18), calls=%async_computation.5 | async-start | bytes 262144 | tf_op jit(solution)/shard_map/all_to_all | solution.py:159
  257.7 2.1 collective-permute-start.12
  260.7 1.2 collective-permute-start.8
  262.0 14.3 %collective-permute-done.11.refs_5_ = bf16[4,8,4096]{2,1,0:T(8,128)(2,1)S(1)} collective-permute-done((bf16[4,8,4096]{2,1,0:T(8,128)(2,1)}, bf16[4,8,4096]{2,1,0:T(8,128)(2,1)S(1)}, u32[]{:S(2)}, u32[]{:S(2)}) %collective-permute-start.11) | collective-permute-done | bytes 262176 | tf_op jit(solution)/shard_map/ppermute | solution.py:154
  276.3 1.0 collective-permute-start.9
  278.6 1.4 collective-permute-start.4
  280.9 4.6 %collective-permute-done.9.refs_3_ = bf16[4,8,4096]{2,1,0:T(8,128)(2,1)S(1)} collective-permute-done((bf16[4,8,4096]{2,1,0:T(8,128)(2,1)}, bf16[4,8,4096]{2,1,0:T(8,128)(2,1)S(1)}, u32[]{:S(2)}, u32[]{:S(2)}) %collective-permute-start.9) | collective-permute-done | bytes 262176 | tf_op jit(solution)/shard_map/ppermute | solution.py:154
  288.3 4.4 %shard_map.85.refs_8_ = bf16[4,32,32768]{2,1,0:T(8,128)(2,1)} custom-call(s32[8]{0:T(128)} %iota_xor_fusion.place_ref, bf16[4,8,4096]{2,1,0:T(8,128)(2,1)} %get-tuple-element.61.refs_0_, bf16[4,8,4096]{2,1,0:T(8,128)(2,1)} %copy-done.19, bf16[4,8,4096]{2,1,0:T(8,128)(2,1)} %copy-done.20, bf16[4,8,4096]{2,1,0:T(8,128)(2,1)} %copy-done.21, ...), custom_call_target="tpu_custom_call" | custom-call | tf_op jit(solution)/shard_map/pallas_call | solution.py:98
  292.7 4.4 %shard_map.86.refs_8_ = bf16[4,32,32768]{2,1,0:T(8,128)(2,1)} custom-call(s32[8]{0:T(128)} %iota_xor_fusion.place_ref, bf16[4,8,4096]{2,1,0:T(8,128)(2,1)} %get-tuple-element.53.refs_0_, bf16[4,8,4096]{2,1,0:T(8,128)(2,1)} %copy-done.3, bf16[4,8,4096]{2,1,0:T(8,128)(2,1)} %copy-done.4, ...), custom_call_target="tpu_custom_call", output_to_operand_aliasing={{}: (9, {})} | custom-call | tf_op jit(solution)/shard_map/pallas_call | solution.py:98
  297.1 4.4 %shard_map.87.refs_8_ = bf16[4,32,32768]{2,1,0:T(8,128)(2,1)} custom-call(s32[8]{0:T(128)} %iota_xor_fusion.place_ref, bf16[4,8,4096]{2,1,0:T(8,128)(2,1)} %get-tuple-element.45.refs_0_, bf16[4,8,4096]{2,1,0:T(8,128)(2,1)} %copy-done.16, bf16[4,8,4096]{2,1,0:T(8,128)(2,1)} %copy-done.17, ...), custom_call_target="tpu_custom_call", output_to_operand_aliasing={{}: (9, {})} | custom-call | tf_op jit(solution)/shard_map/pallas_call | solution.py:98
  301.5 1.8 collective-permute-done.4.refs_5_
  303.4 4.4 %shard_map.88 = bf16[4,32,32768]{2,1,0:T(8,128)(2,1)} custom-call(s32[8]{0:T(128)} %iota_xor_fusion.place_ref, bf16[4,8,4096]{2,1,0:T(8,128)(2,1)} %get-tuple-element.36.refs_0_, bf16[4,8,4096]{2,1,0:T(8,128)(2,1)} %copy-done.9, bf16[4,8,4096]{2,1,0:T(8,128)(2,1)} %copy-done.10, ...), custom_call_target="tpu_custom_call", output_to_operand_aliasing={{}: (9, {})} | custom-call | tf_op jit(solution)/shard_map/pallas_call | solution.py:98
  (131 shorter events, 20.3 us)
Async XLA Ops:
  5.2 11.9 %all-to-all-start.1 = ((s32[32,1,128]{2,1,0:T(1,128)}), s32[32,1,128]{2,1,0:T(1,128)S(1)}, u32[]{:S(2)}, u32[]{:S(2)}) async-start(s32[32,1,128]{2,1,0:T(1,128)} %reshape.175), calls=%async_computation.1 | async-start | bytes 32768 | tf_op jit(solution)/shard_map/all_to_all | solution.py:132
  17.1 52.6 %all-to-all-start.4 = ((bf16[32,8,4096]{2,1,0:T(8,128)(2,1)}), bf16[32,8,4096]{2,1,0:T(8,128)(2,1)S(1)}, u32[]{:S(2)}, u32[]{:S(2)}) async-start(bf16[32,8,4096]{2,1,0:T(8,128)(2,1)} %bitcast.61), calls=%async_computation.4 | async-start | bytes 4194304 | tf_op jit(solution)/shard_map/all_to_all | solution.py:145
  71.1 51.5 %all-to-all-start.3 = ((bf16[32,8,4096]{2,1,0:T(8,128)(2,1)}), bf16[32,8,4096]{2,1,0:T(8,128)(2,1)S(1)}, u32[]{:S(2)}, u32[]{:S(2)}) async-start(bf16[32,8,4096]{2,1,0:T(8,128)(2,1)} %bitcast.62), calls=%async_computation.3 | async-start | bytes 4194304 | tf_op jit(solution)/shard_map/all_to_all | solution.py:145
  123.9 51.5 %all-to-all-start = ((bf16[32,8,4096]{2,1,0:T(8,128)(2,1)}), bf16[32,8,4096]{2,1,0:T(8,128)(2,1)S(1)}, u32[]{:S(2)}, u32[]{:S(2)}) async-start(bf16[32,8,4096]{2,1,0:T(8,128)(2,1)} %bitcast.60), calls=%async_computation | async-start | bytes 4194304 | tf_op jit(solution)/shard_map/all_to_all | solution.py:145
  176.7 59.7 %all-to-all-start.2 = ((bf16[32,8,4096]{2,1,0:T(8,128)(2,1)}), bf16[32,8,4096]{2,1,0:T(8,128)(2,1)}, u32[]{:S(2)}, u32[]{:S(2)}) async-start(bf16[32,8,4096]{2,1,0:T(8,128)(2,1)} %bitcast.59), calls=%async_computation.2 | async-start | bytes 4194304 | tf_op jit(solution)/shard_map/all_to_all | solution.py:145
  187.2 8.9 %collective-permute-start.21 = (bf16[4,8,4096]{2,1,0:T(8,128)(2,1)}, bf16[4,8,4096]{2,1,0:T(8,128)(2,1)S(1)}, u32[]{:S(2)}, u32[]{:S(2)}) collective-permute-start(bf16[4,8,4096]{2,1,0:T(8,128)(2,1)} %get-tuple-element.62), channel_id=1, source_target_pairs={{0,4},{4,0},{8,12},{12,8},{16,20},{20,16},{24,28},{28,24},{1,5},{5... | collective-permute-start | bytes 786440 | tf_op jit(solution)/shard_map/ppermute | solution.py:154
  188.1 13.4 %collective-permute-start.22 = (bf16[4,8,4096]{2,1,0:T(8,128)(2,1)}, bf16[4,8,4096]{2,1,0:T(8,128)(2,1)S(1)}, u32[]{:S(2)}, u32[]{:S(2)}) collective-permute-start(bf16[4,8,4096]{2,1,0:T(8,128)(2,1)} %get-tuple-element.63), channel_id=1, source_target_pairs={{0,8},{4,12},{8,0},{12,4},{16,24},{20,28},{24,16},{28,20},{1,9},{5... | collective-permute-start | bytes 786440 | tf_op jit(solution)/shard_map/ppermute | solution.py:154
  188.9 25.0 %collective-permute-start.23 = (bf16[4,8,4096]{2,1,0:T(8,128)(2,1)}, bf16[4,8,4096]{2,1,0:T(8,128)(2,1)S(1)}, u32[]{:S(2)}, u32[]{:S(2)}) collective-permute-start(bf16[4,8,4096]{2,1,0:T(8,128)(2,1)} %get-tuple-element.64), channel_id=1, source_target_pairs={{0,12},{4,8},{8,4},{12,0},{16,28},{20,24},{24,20},{28,16},{1,13},{... | collective-permute-start | bytes 786440 | tf_op jit(solution)/shard_map/ppermute | solution.py:154
  189.8 24.0 %collective-permute-start.24 = (bf16[4,8,4096]{2,1,0:T(8,128)(2,1)}, bf16[4,8,4096]{2,1,0:T(8,128)(2,1)S(1)}, u32[]{:S(2)}, u32[]{:S(2)}) collective-permute-start(bf16[4,8,4096]{2,1,0:T(8,128)(2,1)} %get-tuple-element.65), channel_id=1, source_target_pairs={{0,16},{4,20},{8,24},{12,28},{16,0},{20,4},{24,8},{28,12},{1,17},{... | collective-permute-start | bytes 786440 | tf_op jit(solution)/shard_map/ppermute | solution.py:154
  190.6 10.9 %copy-start.28 = (bf16[4,8,4096]{2,1,0:T(8,128)(2,1)S(1)}, bf16[4,8,4096]{2,1,0:T(8,128)(2,1)}, u32[]{:S(2)}) copy-start(bf16[4,8,4096]{2,1,0:T(8,128)(2,1)} %get-tuple-element.68) | copy-start | bytes 786436
  190.6 26.8 %collective-permute-start.25 = (bf16[4,8,4096]{2,1,0:T(8,128)(2,1)}, bf16[4,8,4096]{2,1,0:T(8,128)(2,1)S(1)}, u32[]{:S(2)}, u32[]{:S(2)}) collective-permute-start(bf16[4,8,4096]{2,1,0:T(8,128)(2,1)} %get-tuple-element.66), channel_id=1, source_target_pairs={{0,20},{4,16},{8,28},{12,24},{16,4},{20,0},{24,12},{28,8},{1,21},{... | collective-permute-start | bytes 786440 | tf_op jit(solution)/shard_map/ppermute | solution.py:154
  196.1 40.3 %copy-start.19 = (bf16[4,8,4096]{2,1,0:T(8,128)(2,1)}, bf16[4,8,4096]{2,1,0:T(8,128)(2,1)S(1)}, u32[]{:S(2)}) copy-start(bf16[4,8,4096]{2,1,0:T(8,128)(2,1)S(1)} %collective-permute-done.21.refs_1_) | copy-start | bytes 786436
  196.1 25.7 %collective-permute-start.26 = (bf16[4,8,4096]{2,1,0:T(8,128)(2,1)S(1)}, bf16[4,8,4096]{2,1,0:T(8,128)(2,1)S(1)}, u32[]{:S(2)}, u32[]{:S(2)}) collective-permute-start(bf16[4,8,4096]{2,1,0:T(8,128)(2,1)S(1)} %copy-done.30), channel_id=1, source_target_pairs={{0,24},{4,28},{8,16},{12,20},{16,8},{20,12},{24,0},{28,4},{1,25},{... | collective-permute-start | bytes 786440 | tf_op jit(solution)/shard_map/ppermute | solution.py:154
  201.5 12.3 %copy-start.20 = (bf16[4,8,4096]{2,1,0:T(8,128)(2,1)}, bf16[4,8,4096]{2,1,0:T(8,128)(2,1)S(1)}, u32[]{:S(2)}) copy-start(bf16[4,8,4096]{2,1,0:T(8,128)(2,1)S(1)} %collective-permute-done.22.refs_2_) | copy-start | bytes 786436
  201.5 28.8 %collective-permute-start.27 = (bf16[4,8,4096]{2,1,0:T(8,128)(2,1)S(1)}, bf16[4,8,4096]{2,1,0:T(8,128)(2,1)S(1)}, u32[]{:S(2)}, u32[]{:S(2)}) collective-permute-start(bf16[4,8,4096]{2,1,0:T(8,128)(2,1)S(1)} %copy-done.28), channel_id=1, source_target_pairs={{0,28},{4,24},{8,20},{12,16},{16,12},{20,8},{24,4},{28,0},{1,29},{... | collective-permute-start | bytes 786440 | tf_op jit(solution)/shard_map/ppermute | solution.py:154
  213.9 16.5 %collective-permute-start.14 = (bf16[4,8,4096]{2,1,0:T(8,128)(2,1)}, bf16[4,8,4096]{2,1,0:T(8,128)(2,1)S(1)}, u32[]{:S(2)}, u32[]{:S(2)}) collective-permute-start(bf16[4,8,4096]{2,1,0:T(8,128)(2,1)} %get-tuple-element.54), channel_id=1, source_target_pairs={{0,4},{4,0},{8,12},{12,8},{16,20},{20,16},{24,28},{28,24},{1,5},{5... | collective-permute-start | bytes 786440 | tf_op jit(solution)/shard_map/ppermute | solution.py:154
  214.6 26.4 %collective-permute-start.15 = (bf16[4,8,4096]{2,1,0:T(8,128)(2,1)}, bf16[4,8,4096]{2,1,0:T(8,128)(2,1)S(1)}, u32[]{:S(2)}, u32[]{:S(2)}) collective-permute-start(bf16[4,8,4096]{2,1,0:T(8,128)(2,1)} %get-tuple-element.55), channel_id=1, source_target_pairs={{0,8},{4,12},{8,0},{12,4},{16,24},{20,28},{24,16},{28,20},{1,9},{5... | collective-permute-start | bytes 786440 | tf_op jit(solution)/shard_map/ppermute | solution.py:154
  217.4 25.5 %collective-permute-start.16 = (bf16[4,8,4096]{2,1,0:T(8,128)(2,1)}, bf16[4,8,4096]{2,1,0:T(8,128)(2,1)S(1)}, u32[]{:S(2)}, u32[]{:S(2)}) collective-permute-start(bf16[4,8,4096]{2,1,0:T(8,128)(2,1)} %get-tuple-element.56), channel_id=1, source_target_pairs={{0,12},{4,8},{8,4},{12,0},{16,28},{20,24},{24,20},{28,16},{1,13},{... | collective-permute-start | bytes 786440 | tf_op jit(solution)/shard_map/ppermute | solution.py:154
  221.8 21.2 %collective-permute-start.17 = (bf16[4,8,4096]{2,1,0:T(8,128)(2,1)}, bf16[4,8,4096]{2,1,0:T(8,128)(2,1)S(1)}, u32[]{:S(2)}, u32[]{:S(2)}) collective-permute-start(bf16[4,8,4096]{2,1,0:T(8,128)(2,1)} %get-tuple-element.57), channel_id=1, source_target_pairs={{0,16},{4,20},{8,24},{12,28},{16,0},{20,4},{24,8},{28,12},{1,17},{... | collective-permute-start | bytes 786440 | tf_op jit(solution)/shard_map/ppermute | solution.py:154
  230.3 13.6 %collective-permute-start.18 = (bf16[4,8,4096]{2,1,0:T(8,128)(2,1)}, bf16[4,8,4096]{2,1,0:T(8,128)(2,1)S(1)}, u32[]{:S(2)}, u32[]{:S(2)}) collective-permute-start(bf16[4,8,4096]{2,1,0:T(8,128)(2,1)} %get-tuple-element.58), channel_id=1, source_target_pairs={{0,20},{4,16},{8,28},{12,24},{16,4},{20,0},{24,12},{28,8},{1,21},{... | collective-permute-start | bytes 786440 | tf_op jit(solution)/shard_map/ppermute | solution.py:154
  231.0 15.3 %collective-permute-start.19 = (bf16[4,8,4096]{2,1,0:T(8,128)(2,1)}, bf16[4,8,4096]{2,1,0:T(8,128)(2,1)S(1)}, u32[]{:S(2)}, u32[]{:S(2)}) collective-permute-start(bf16[4,8,4096]{2,1,0:T(8,128)(2,1)} %get-tuple-element.59), channel_id=1, source_target_pairs={{0,24},{4,28},{8,16},{12,20},{16,8},{20,12},{24,0},{28,4},{1,25},{... | collective-permute-start | bytes 786440 | tf_op jit(solution)/shard_map/ppermute | solution.py:154
  241.0 46.3 %copy-start.4 = (bf16[4,8,4096]{2,1,0:T(8,128)(2,1)}, bf16[4,8,4096]{2,1,0:T(8,128)(2,1)S(1)}, u32[]{:S(2)}) copy-start(bf16[4,8,4096]{2,1,0:T(8,128)(2,1)S(1)} %collective-permute-done.15.refs_2_) | copy-start | bytes 786436
  241.0 16.6 %collective-permute-start.20 = (bf16[4,8,4096]{2,1,0:T(8,128)(2,1)S(1)}, bf16[4,8,4096]{2,1,0:T(8,128)(2,1)S(1)}, u32[]{:S(2)}, u32[]{:S(2)}) collective-permute-start(bf16[4,8,4096]{2,1,0:T(8,128)(2,1)S(1)} %copy-done.27), channel_id=1, source_target_pairs={{0,28},{4,24},{8,20},{12,16},{16,12},{20,8},{24,4},{28,0},{1,29},{... | collective-permute-start | bytes 786440 | tf_op jit(solution)/shard_map/ppermute | solution.py:154
  243.0 44.4 %copy-start.5 = (bf16[4,8,4096]{2,1,0:T(8,128)(2,1)}, bf16[4,8,4096]{2,1,0:T(8,128)(2,1)S(1)}, u32[]{:S(2)}) copy-start(bf16[4,8,4096]{2,1,0:T(8,128)(2,1)S(1)} %collective-permute-done.16.refs_3_) | copy-start | bytes 786436
  243.0 16.9 %collective-permute-start = (bf16[4,8,4096]{2,1,0:T(8,128)(2,1)S(1)}, bf16[4,8,4096]{2,1,0:T(8,128)(2,1)S(1)}, u32[]{:S(2)}, u32[]{:S(2)}) collective-permute-start(bf16[4,8,4096]{2,1,0:T(8,128)(2,1)S(1)} %copy-done.29), channel_id=1, source_target_pairs={{0,4},{4,0},{8,12},{12,8},{16,20},{20,16},{24,28},{28,24},{1,5},{5... | collective-permute-start | bytes 786440 | tf_op jit(solution)/shard_map/ppermute | solution.py:154
  243.0 44.3 %copy-start.6 = (bf16[4,8,4096]{2,1,0:T(8,128)(2,1)}, bf16[4,8,4096]{2,1,0:T(8,128)(2,1)S(1)}, u32[]{:S(2)}) copy-start(bf16[4,8,4096]{2,1,0:T(8,128)(2,1)S(1)} %collective-permute-done.17.refs_4_) | copy-start | bytes 786436
  243.1 17.6 %collective-permute-start.1 = (bf16[4,8,4096]{2,1,0:T(8,128)(2,1)}, bf16[4,8,4096]{2,1,0:T(8,128)(2,1)S(1)}, u32[]{:S(2)}, u32[]{:S(2)}) collective-permute-start(bf16[4,8,4096]{2,1,0:T(8,128)(2,1)} %get-tuple-element.38), channel_id=1, source_target_pairs={{0,8},{4,12},{8,0},{12,4},{16,24},{20,28},{24,16},{28,20},{1,9},{5... | collective-permute-start | bytes 786440 | tf_op jit(solution)/shard_map/ppermute | solution.py:154
  244.0 43.4 %copy-start.7 = (bf16[4,8,4096]{2,1,0:T(8,128)(2,1)}, bf16[4,8,4096]{2,1,0:T(8,128)(2,1)S(1)}, u32[]{:S(2)}) copy-start(bf16[4,8,4096]{2,1,0:T(8,128)(2,1)S(1)} %collective-permute-done.18.refs_5_) | copy-start | bytes 786436
  244.0 16.7 %collective-permute-start.10 = (bf16[4,8,4096]{2,1,0:T(8,128)(2,1)}, bf16[4,8,4096]{2,1,0:T(8,128)(2,1)S(1)}, u32[]{:S(2)}, u32[]{:S(2)}) collective-permute-start(bf16[4,8,4096]{2,1,0:T(8,128)(2,1)} %get-tuple-element.49), channel_id=1, source_target_pairs={{0,16},{4,20},{8,24},{12,28},{16,0},{20,4},{24,8},{28,12},{1,17},{... | collective-permute-start | bytes 786440 | tf_op jit(solution)/shard_map/ppermute | solution.py:154
  246.3 41.1 %copy-start.8 = (bf16[4,8,4096]{2,1,0:T(8,128)(2,1)}, bf16[4,8,4096]{2,1,0:T(8,128)(2,1)S(1)}, u32[]{:S(2)}) copy-start(bf16[4,8,4096]{2,1,0:T(8,128)(2,1)S(1)} %collective-permute-done.19.refs_6_) | copy-start | bytes 786436
  246.3 30.0 %collective-permute-start.11 = (bf16[4,8,4096]{2,1,0:T(8,128)(2,1)}, bf16[4,8,4096]{2,1,0:T(8,128)(2,1)S(1)}, u32[]{:S(2)}, u32[]{:S(2)}) collective-permute-start(bf16[4,8,4096]{2,1,0:T(8,128)(2,1)} %get-tuple-element.50), channel_id=1, source_target_pairs={{0,20},{4,16},{8,28},{12,24},{16,4},{20,0},{24,12},{28,8},{1,21},{... | collective-permute-start | bytes 786440 | tf_op jit(solution)/shard_map/ppermute | solution.py:154
  248.2 38.5 %all-to-all-start.5 = ((f32[1,128,256]{1,0,2:T(1,128)}), f32[1,128,256]{1,0,2:T(1,128)S(1)}, u32[]{:S(2)}, u32[]{:S(2)}) async-start(f32[1,128,256]{1,0,2:T(1,128)} %bitcast.18), calls=%async_computation.5 | async-start | bytes 262144 | tf_op jit(solution)/shard_map/all_to_all | solution.py:159
  257.7 29.7 %copy-start.11 = (bf16[4,8,4096]{2,1,0:T(8,128)(2,1)}, bf16[4,8,4096]{2,1,0:T(8,128)(2,1)S(1)}, u32[]{:S(2)}) copy-start(bf16[4,8,4096]{2,1,0:T(8,128)(2,1)S(1)} %collective-permute-done.20.refs_7_) | copy-start | bytes 786436
  257.7 19.7 %collective-permute-start.12 = (bf16[4,8,4096]{2,1,0:T(8,128)(2,1)}, bf16[4,8,4096]{2,1,0:T(8,128)(2,1)S(1)}, u32[]{:S(2)}, u32[]{:S(2)}) collective-permute-start(bf16[4,8,4096]{2,1,0:T(8,128)(2,1)} %get-tuple-element.51), channel_id=1, source_target_pairs={{0,24},{4,28},{8,16},{12,20},{16,8},{20,12},{24,0},{28,4},{1,25},{... | collective-permute-start | bytes 786440 | tf_op jit(solution)/shard_map/ppermute | solution.py:154
  259.8 27.6 %copy-start.9 = (bf16[4,8,4096]{2,1,0:T(8,128)(2,1)}, bf16[4,8,4096]{2,1,0:T(8,128)(2,1)S(1)}, u32[]{:S(2)}) copy-start(bf16[4,8,4096]{2,1,0:T(8,128)(2,1)S(1)} %collective-permute-done.refs_1_) | copy-start | bytes 786436
  259.8 18.3 %collective-permute-start.13 = (bf16[4,8,4096]{2,1,0:T(8,128)(2,1)}, bf16[4,8,4096]{2,1,0:T(8,128)(2,1)S(1)}, u32[]{:S(2)}, u32[]{:S(2)}) collective-permute-start(bf16[4,8,4096]{2,1,0:T(8,128)(2,1)} %get-tuple-element.52), channel_id=1, source_target_pairs={{0,28},{4,24},{8,20},{12,16},{16,12},{20,8},{24,4},{28,0},{1,29},{... | collective-permute-start | bytes 786440 | tf_op jit(solution)/shard_map/ppermute | solution.py:154
  260.7 26.7 %copy-start.10 = (bf16[4,8,4096]{2,1,0:T(8,128)(2,1)}, bf16[4,8,4096]{2,1,0:T(8,128)(2,1)S(1)}, u32[]{:S(2)}) copy-start(bf16[4,8,4096]{2,1,0:T(8,128)(2,1)S(1)} %collective-permute-done.1.refs_2_) | copy-start | bytes 786436
  260.7 17.9 %collective-permute-start.7 = (bf16[4,8,4096]{2,1,0:T(8,128)(2,1)}, bf16[4,8,4096]{2,1,0:T(8,128)(2,1)S(1)}, u32[]{:S(2)}, u32[]{:S(2)}) collective-permute-start(bf16[4,8,4096]{2,1,0:T(8,128)(2,1)} %get-tuple-element.46), channel_id=1, source_target_pairs={{0,4},{4,0},{8,12},{12,8},{16,20},{20,16},{24,28},{28,24},{1,5},{5... | collective-permute-start | bytes 786440 | tf_op jit(solution)/shard_map/ppermute | solution.py:154
  260.7 26.7 %copy-start.12 = (bf16[4,8,4096]{2,1,0:T(8,128)(2,1)}, bf16[4,8,4096]{2,1,0:T(8,128)(2,1)S(1)}, u32[]{:S(2)}) copy-start(bf16[4,8,4096]{2,1,0:T(8,128)(2,1)S(1)} %collective-permute-done.10.refs_4_) | copy-start | bytes 786436
  260.7 19.3 %collective-permute-start.8 = (bf16[4,8,4096]{2,1,0:T(8,128)(2,1)}, bf16[4,8,4096]{2,1,0:T(8,128)(2,1)S(1)}, u32[]{:S(2)}, u32[]{:S(2)}) collective-permute-start(bf16[4,8,4096]{2,1,0:T(8,128)(2,1)} %get-tuple-element.47), channel_id=1, source_target_pairs={{0,8},{4,12},{8,0},{12,4},{16,24},{20,28},{24,16},{28,20},{1,9},{5... | collective-permute-start | bytes 786440 | tf_op jit(solution)/shard_map/ppermute | solution.py:154
  276.3 11.1 %copy-start.13 = (bf16[4,8,4096]{2,1,0:T(8,128)(2,1)}, bf16[4,8,4096]{2,1,0:T(8,128)(2,1)S(1)}, u32[]{:S(2)}) copy-start(bf16[4,8,4096]{2,1,0:T(8,128)(2,1)S(1)} %collective-permute-done.11.refs_5_) | copy-start | bytes 786436
  276.3 9.2 %collective-permute-start.9 = (bf16[4,8,4096]{2,1,0:T(8,128)(2,1)}, bf16[4,8,4096]{2,1,0:T(8,128)(2,1)S(1)}, u32[]{:S(2)}, u32[]{:S(2)}) collective-permute-start(bf16[4,8,4096]{2,1,0:T(8,128)(2,1)} %get-tuple-element.48), channel_id=1, source_target_pairs={{0,12},{4,8},{8,4},{12,0},{16,28},{20,24},{24,20},{28,16},{1,13},{... | collective-permute-start | bytes 786440 | tf_op jit(solution)/shard_map/ppermute | solution.py:154
  277.4 10.1 %copy-start.14 = (bf16[4,8,4096]{2,1,0:T(8,128)(2,1)}, bf16[4,8,4096]{2,1,0:T(8,128)(2,1)S(1)}, u32[]{:S(2)}) copy-start(bf16[4,8,4096]{2,1,0:T(8,128)(2,1)S(1)} %collective-permute-done.12.refs_6_) | copy-start | bytes 786436
  277.4 24.2 %collective-permute-start.2 = (bf16[4,8,4096]{2,1,0:T(8,128)(2,1)}, bf16[4,8,4096]{2,1,0:T(8,128)(2,1)}, u32[]{:S(2)}, u32[]{:S(2)}) collective-permute-start(bf16[4,8,4096]{2,1,0:T(8,128)(2,1)} %get-tuple-element.39), channel_id=1, source_target_pairs={{0,12},{4,8},{8,4},{12,0},{16,28},{20,24},{24,20},{28,16},{1,13},{... | collective-permute-start | bytes 786440 | tf_op jit(solution)/shard_map/ppermute | solution.py:154
  278.2 23.4 %collective-permute-start.3 = (bf16[4,8,4096]{2,1,0:T(8,128)(2,1)}, bf16[4,8,4096]{2,1,0:T(8,128)(2,1)}, u32[]{:S(2)}, u32[]{:S(2)}) collective-permute-start(bf16[4,8,4096]{2,1,0:T(8,128)(2,1)} %get-tuple-element.40), channel_id=1, source_target_pairs={{0,16},{4,20},{8,24},{12,28},{16,0},{20,4},{24,8},{28,12},{1,17},{... | collective-permute-start | bytes 786440 | tf_op jit(solution)/shard_map/ppermute | solution.py:154
  278.6 24.7 %collective-permute-start.4 = (bf16[4,8,4096]{2,1,0:T(8,128)(2,1)}, bf16[4,8,4096]{2,1,0:T(8,128)(2,1)}, u32[]{:S(2)}, u32[]{:S(2)}) collective-permute-start(bf16[4,8,4096]{2,1,0:T(8,128)(2,1)} %get-tuple-element.41), channel_id=1, source_target_pairs={{0,20},{4,16},{8,28},{12,24},{16,4},{20,0},{24,12},{28,8},{1,21},{... | collective-permute-start | bytes 786440 | tf_op jit(solution)/shard_map/ppermute | solution.py:154
  280.0 23.3 %collective-permute-start.5 = (bf16[4,8,4096]{2,1,0:T(8,128)(2,1)}, bf16[4,8,4096]{2,1,0:T(8,128)(2,1)}, u32[]{:S(2)}, u32[]{:S(2)}) collective-permute-start(bf16[4,8,4096]{2,1,0:T(8,128)(2,1)} %get-tuple-element.42), channel_id=1, source_target_pairs={{0,24},{4,28},{8,16},{12,20},{16,8},{20,12},{24,0},{28,4},{1,25},{... | collective-permute-start | bytes 786440 | tf_op jit(solution)/shard_map/ppermute | solution.py:154
  285.5 17.8 %collective-permute-start.6 = (bf16[4,8,4096]{2,1,0:T(8,128)(2,1)}, bf16[4,8,4096]{2,1,0:T(8,128)(2,1)}, u32[]{:S(2)}, u32[]{:S(2)}) collective-permute-start(bf16[4,8,4096]{2,1,0:T(8,128)(2,1)} %get-tuple-element.43), channel_id=1, source_target_pairs={{0,28},{4,24},{8,20},{12,16},{16,12},{20,8},{24,4},{28,0},{1,29},{... | collective-permute-start | bytes 786440 | tf_op jit(solution)/shard_map/ppermute | solution.py:154
  (18 other events, 77.5 us)

commit v2 on v1

--- a/solution.py
+++ b/solution.py
@@ -16,16 +16,25 @@
     return jnp.sum(jnp.where(permutation[None, :] == down, across, 0), axis=1)
 
 
-def pool_rows(table_cols, marked):
-    columns = table_cols.shape[0]
-    safe_ids = jnp.maximum(marked, 0).reshape(-1)
-    weights = (marked >= 0).astype(jnp.float32)
-    picked = (
-        jnp.take(table_cols, safe_ids, axis=1)
-        .reshape(columns, marked.shape[0], marked.shape[1])
-        .astype(jnp.float32)
-    )
-    return jnp.sum(picked * weights[None, :, :], axis=2)
+def pool_rows(table_rows_first, marks, bag_size):
+    safe_ids = jnp.maximum(marks - 1, 0)
+    weights = (marks > 0).astype(jnp.float32).reshape(-1, bag_size)
+    picked = jnp.take(table_rows_first, safe_ids, axis=0).astype(jnp.float32)
+    picked = picked.reshape(-1, bag_size, picked.shape[1])
+    return jnp.sum(picked * weights[:, :, None], axis=1)
+
+
+def write_marks(marks, height, dtype):
+    count = marks.shape[0]
+    flat = jnp.concatenate([marks >> 8, marks & 255], axis=1).astype(dtype)
+    lanes = -(-flat.shape[1] // (height * 128)) * 128
+    flat = jnp.pad(flat, ((0, 0), (0, height * lanes - flat.shape[1])))
+    return flat.reshape(count, height, lanes)
+
+
+def read_marks(sent, length):
+    flat = sent.reshape(sent.shape[0], -1).astype(jnp.int32)
+    return flat[:, :length] * 256 + flat[:, length:2 * length]
 
 
 def split_chunk(table, slot, plan, used_rows, chunk, group_count, col_count):
@@ -62,8 +71,8 @@
     return [(own, peer(own, shift, group_count)) for own in range(group_count)]
 
 
-def pick_blocks(blocks, source_slot, group_count, per_group):
-    _, height, block = blocks.shape
+def pick_blocks(blocks, source_slot, group_count, per_group, block):
+    height = blocks.shape[1]
 
     def kernel(slot_ref, *refs):
         for k in range(group_count):
@@ -127,13 +136,13 @@
     for k in range(CHUNKS):
         pieces.append(split_chunk(table, slot, old_plan, table_rows, k, group_count, col_count))
     bag_iota = lax.broadcasted_iota(jnp.int32, (1, 1, bag_size), 2)
-    marked = jnp.where(bag_iota < bag_len[:, :, None], ids, -1)
-    by_slot = jnp.take(marked, old_plan, axis=1)
-    own_ids = lax.all_to_all(
-        by_slot, ("grp", "col"), split_axis=1, concat_axis=0, tiled=True
-    ).reshape(-1, bag_size)
-    partial_value = pool_rows(table, own_ids)
-    pieces[2], partial_value = lax.optimization_barrier((pieces[2], partial_value))
+    marked = jnp.where(bag_iota < bag_len[:, :, None], ids + 1, 0)
+    own_batch = marked.shape[0]
+    by_slot = jnp.transpose(jnp.take(marked, old_plan, axis=1), (1, 0, 2)).reshape(device_count, -1)
+    assert table_len <= 65536
+    marks_out = write_marks(by_slot, height, table.dtype)
+    turned = lax.optimization_barrier(jnp.transpose(table))
+    pieces[2], turned = lax.optimization_barrier((pieces[2], turned))
     old_inverse = invert(old_plan)
     source_slot = old_inverse[new_plan]
     own_group = lax.axis_index("grp").astype(jnp.int32)
@@ -142,14 +151,21 @@
     by_peer = source_slot.reshape(group_count, per_group)[sources].reshape(-1)
     new_local = None
     for k in range(CHUNKS):
+        leaving = pieces[k].reshape(device_count, height, row_block)
+        if k == 1:
+            leaving = jnp.concatenate([leaving, marks_out], axis=2)
         got = lax.all_to_all(
-            pieces[k].reshape(device_count, height, row_block),
+            leaving,
             ("grp", "col"),
             split_axis=0,
             concat_axis=0,
             tiled=True,
         )
-        send = pick_blocks(got, by_peer, group_count, per_group)
+        if k == 1:
+            marks = read_marks(got[:, :, row_block:], own_batch * bag_size).reshape(-1)
+            partial_value = pool_rows(turned, marks, bag_size)
+            pieces[3], partial_value = lax.optimization_barrier((pieces[3], partial_value))
+        send = pick_blocks(got, by_peer, group_count, per_group, row_block)
         landed = [send[0]] + [
             lax.ppermute(send[shift], "grp", peer_pairs(shift, group_count))
             for shift in range(1, group_count)
@@ -157,14 +173,13 @@
         new_local = join_chunk(landed, places, new_local, k)
 
     returned = lax.all_to_all(
-        partial_value.reshape(1, full_width, -1),
+        partial_value.reshape(device_count, own_batch, full_width),
         ("grp", "col"),
-        split_axis=2,
+        split_axis=0,
         concat_axis=0,
         tiled=True,
     )
-    by_table = jnp.take(returned, old_inverse, axis=0)
-    pooled = jnp.transpose(by_table, (2, 0, 1))
+    pooled = jnp.transpose(jnp.take(returned, old_inverse, axis=0), (1, 0, 2))
     return (new_local, pooled)
 
 

time: 313 us -> 309 us (0.987)
  local copies, waits for them, and re-layouts: 40.2 us -> 34.2 us
    squeeze x1 -> x0, local copies, waits for them, and re-layouts: 11.9 us -> none  [move(): table = old_tables[0]]
    optimization_barrier x0 -> x1, local copies, waits for them, and re-layouts: none -> 11.9 us  [move(): pieces[2], turned = lax.optimization_barrier((pieces[2], turned))]
    ppermute x28, starting transfers between devices: 25.3 us -> 36.9 us  [move(): lax.ppermute(send[shift], 'grp', peer_pairs(shift, group_count))]
    all_to_all x6 -> x5, starting transfers between devices: 32.1 us -> 23 us  [the longest x4 17.9 us: move(): lax.all_to_all(leaving, ('grp', 'col'), split_axis=0, concat_axis=0, tile...]
    unnamed x69 -> x67, local copies, waits for them, and re-layouts: 9.02 us -> 3.27 us
    all_to_all x6 -> x5, waiting for transfers between devices: 99 us -> 96.1 us  [the longest x4 96.1 us: move(): lax.all_to_all(leaving, ('grp', 'col'), split_axis=0, concat_axis=0, tile...]
    gather x3 -> x4, local copies, waits for them, and re-layouts: 16.7 us -> 16.7 us  [the longest x1 15.5 us: pool_rows(): picked = jnp.take(table_rows_first, safe_ids, axis=0).astype(jnp.float32)]
  transfers between devices with their start and end apart: 34 -> 33, of which waited for: 13 -> 13; matrix products, arithmetic and copies ran while one was open for 11% -> 12% of each run, Pallas kernels for 16% -> 15%
where the time goes in v2:
time: 309 us; the launch traced here: 305 us
  waiting for transfers between devices  150 us (49%)
  starting transfers between devices  59.9 us (19%)
  Pallas kernels  54 us (17%)
  local copies, waits for them, and re-layouts  34.2 us (11%)
  other arithmetic  6.29 us (2%)
    all_to_all x4, waiting for transfers between devices, move(): lax.all_to_all(leaving, ('grp', 'col'), split_axis=0, concat_axis=0, tile...  96.1 us
    ppermute x28, waiting for transfers between devices, move(): lax.ppermute(send[shift], 'grp', peer_pairs(shift, group_count))  53.6 us
    ppermute x28, starting transfers between devices, move(): lax.ppermute(send[shift], 'grp', peer_pairs(shift, group_count))  36.9 us
    pallas_call x4, Pallas kernels, split_chunk(): pl.pallas_call(kernel, grid_spec=pltpu.PrefetchScalarGridSpec(num_scalar_...  18.6 us
    all_to_all x4, starting transfers between devices, move(): lax.all_to_all(leaving, ('grp', 'col'), split_axis=0, concat_axis=0, tile...  17.9 us
    pallas_call x4, Pallas kernels, pick_blocks(): pl.pallas_call(kernel, grid_spec=pltpu.PrefetchScalarGridSpec(num_scalar_...  17.7 us
    pallas_call x4, Pallas kernels, join_chunk(): pl.pallas_call(kernel, grid_spec=pltpu.PrefetchScalarGridSpec(num_scalar_...  17.7 us
    gather x1, local copies, waits for them, and re-layouts, pool_rows(): picked = jnp.take(table_rows_first, safe_ids, axis=0).astype(jnp.float32)  15.5 us
  transfers between devices with their start and end apart: 33, of which 13 were waited for; matrix products, arithmetic and copies ran while one was open for 12% of the time, Pallas kernels for 15%

profile of v2, /device:TPU:9, one launch (start us, length us, event | category | flops | bytes accessed | tf_op | source)
XLA Modules:
  0.0 305.3 jit_solution(6255644153306811831)
XLA Ops:
  0.6 4.6 %shard_map.83 = bf16[8,4,8,4096]{3,2,1,0:T(8,128)(2,1)} custom-call(s32[1]{0:T(128)} %bitcast.1.slot_ref, s32[32]{0:T(128)} %plan_ref.7, s32[32]{0:T(128)} %used_ref.7, bf16[128,32768]{1,0:T(8,128)(2,1)} %bitcast.30), custom_call_target="tpu_custom_call" | custom-call | tf_op jit(solution)/shard_map/pallas_call | solution.py:52
  5.3 6.3 %all-to-all-start.3 = ((bf16[32,8,4096]{2,1,0:T(8,128)(2,1)}), bf16[32,8,4096]{2,1,0:T(8,128)(2,1)S(1)}, u32[]{:S(2)}, u32[]{:S(2)}) async-start(bf16[32,8,4096]{2,1,0:T(8,128)(2,1)} %bitcast.36), calls=%async_computation.3 | async-start | bytes 4194304 | tf_op jit(solution)/shard_map/all_to_all | solution.py:157
  11.6 4.8 %shard_map.78 = bf16[8,4,8,4096]{3,2,1,0:T(8,128)(2,1)} custom-call(s32[1]{0:T(128)} %bitcast.1.slot_ref, s32[32]{0:T(128)} %plan_ref.7, s32[32]{0:T(128)} %used_ref.7, bf16[128,32768]{1,0:T(8,128)(2,1)} %bitcast.31), custom_call_target="tpu_custom_call" | custom-call | tf_op jit(solution)/shard_map/pallas_call | solution.py:52
  17.7 3.1 %pad_maximum_fusion = bf16[32,8,4224]{2,1,0:T(8,128)(2,1)} fusion(bf16[32,8,128]{2,1,0:T(8,128)(2,1)S(1)} %bitcast.42, bf16[32,8,4096]{2,1,0:T(8,128)(2,1)} %bitcast.38), kind=kLoop, calls=%fused_computation.5 | loop fusion | flops 4325376 | bytes 4325376 | tf_op jit(solution)/shard_map/concatenate | solution.py:156
  20.8 38.5 %all-to-all-done.3.refs_0_.refs_1_.refs_2_.refs_3_.refs_4_.refs_5_.refs_6_.refs_7_ = bf16[32,8,4096]{2,1,0:T(8,128)(2,1)S(1)} async-done(((bf16[32,8,4096]{2,1,0:T(8,128)(2,1)}), bf16[32,8,4096]{2,1,0:T(8,128)(2,1)S(1)}, u32[]{:S(2)}, u32[]{:S(2)}) %all-to-all-start.3) | async-done | bytes 2097184 | tf_op jit(solution)/shard_map/all_to_all | solution.py:157
  59.3 1.4 copy-done.2
  60.7 3.8 %all-to-all-start = ((bf16[32,8,4224]{2,1,0:T(8,128)(2,1)}), bf16[32,8,4224]{2,1,0:T(8,128)(2,1)S(1)}, u32[]{:S(2)}, u32[]{:S(2)}) async-start(bf16[32,8,4224]{2,1,0:T(8,128)(2,1)} %pad_maximum_fusion), calls=%async_computation | async-start | bytes 4325376 | tf_op jit(solution)/shard_map/all_to_all | solution.py:157
  64.5 4.6 %shard_map.79 = bf16[8,4,8,4096]{3,2,1,0:T(8,128)(2,1)} custom-call(s32[1]{0:T(128)} %bitcast.1.slot_ref, s32[32]{0:T(128)} %plan_ref.7, s32[32]{0:T(128)} %used_ref.7, bf16[128,32768]{1,0:T(8,128)(2,1)} %bitcast.32), custom_call_target="tpu_custom_call" | custom-call | tf_op jit(solution)/shard_map/pallas_call | solution.py:52
  69.1 44.6 %all-to-all-done.refs_0_.refs_1_.refs_2_.refs_3_.refs_4_.refs_5_.refs_6_.refs_7_ = bf16[32,8,4224]{2,1,0:T(8,128)(2,1)S(1)} async-done(((bf16[32,8,4224]{2,1,0:T(8,128)(2,1)}), bf16[32,8,4224]{2,1,0:T(8,128)(2,1)S(1)}, u32[]{:S(2)}, u32[]{:S(2)}) %all-to-all-start) | async-done | bytes 2162720 | tf_op jit(solution)/shard_map/all_to_all | solution.py:157
  113.7 3.7 %all-to-all-start.2 = ((bf16[32,8,4096]{2,1,0:T(8,128)(2,1)}), bf16[32,8,4096]{2,1,0:T(8,128)(2,1)}, u32[]{:S(2)}, u32[]{:S(2)}) async-start(bf16[32,8,4096]{2,1,0:T(8,128)(2,1)} %bitcast.37), calls=%async_computation.2 | async-start | bytes 4194304 | tf_op jit(solution)/shard_map/all_to_all | solution.py:157
  117.4 4.6 %shard_map.77 = bf16[8,4,8,4096]{3,2,1,0:T(8,128)(2,1)} custom-call(s32[1]{0:T(128)} %bitcast.1.slot_ref, s32[32]{0:T(128)} %plan_ref.7, s32[32]{0:T(128)} %used_ref.7, bf16[128,32768]{1,0:T(8,128)(2,1)} %bitcast.33), custom_call_target="tpu_custom_call" | custom-call | tf_op jit(solution)/shard_map/pallas_call | solution.py:52
  122.0 11.9 %copy.46 = bf16[32768,128]{1,0:T(8,128)(2,1)} copy(bf16[32768,128]{0,1:T(8,128)(2,1)} %bitcast.34) | data formatting | bytes 16777216 | tf_op jit(solution)/shard_map/optimization_barrier | solution.py:145
  134.2 15.5 %gather_fusion.3 = bf16[4096,128]{1,0:T(8,128)(2,1)S(1)} fusion(bf16[32768,128]{1,0:T(8,128)(2,1)} %copy.46, s32[4096]{0:T(1024)S(1)} %bitcast_clamp_fusion), kind=kCustom, calls=%fused_computation.3 | custom fusion | bytes 2113536 | tf_op jit(solution)/shard_map/jit(_take)/gather | solution.py:22
  149.7 2.2 multiply_reduce_fusion
  151.9 13.0 %all-to-all-done.2.refs_0_.refs_1_.refs_2_.refs_3_.refs_4_.refs_5_.refs_6_.refs_7_ = bf16[32,8,4096]{2,1,0:T(8,128)(2,1)} async-done(((bf16[32,8,4096]{2,1,0:T(8,128)(2,1)}), bf16[32,8,4096]{2,1,0:T(8,128)(2,1)}, u32[]{:S(2)}, u32[]{:S(2)}) %all-to-all-start.2) | async-done | bytes 2097184 | tf_op jit(solution)/shard_map/all_to_all | solution.py:157
  164.9 4.1 %all-to-all-start.1 = ((bf16[32,8,4096]{2,1,0:T(8,128)(2,1)}), bf16[32,8,4096]{2,1,0:T(8,128)(2,1)S(1)}, u32[]{:S(2)}, u32[]{:S(2)}) async-start(bf16[32,8,4096]{2,1,0:T(8,128)(2,1)} %bitcast.35), calls=%async_computation.1 | async-start | bytes 4194304 | tf_op jit(solution)/shard_map/all_to_all | solution.py:157
  171.2 4.4 %shard_map.84 = (bf16[4,8,4096]{2,1,0:T(8,128)(2,1)}, bf16[4,8,4096]{2,1,0:T(8,128)(2,1)}, bf16[4,8,4096]{2,1,0:T(8,128)(2,1)}, bf16[4,8,4096]{2,1,0:T(8,128)(2,...) custom-call(s32[32]{0:T(128)} %reshape.130.slot_ref, ...), custom_call_target="tpu_custom_call" | custom-call | tf_op jit(solution)/shard_map/pallas_call | solution.py:84
  176.1 1.2 collective-permute-start.22
  177.8 1.2 collective-permute-start.24
  179.6 4.4 %shard_map.81 = (bf16[4,8,4096]{2,1,0:T(8,128)(2,1)}, bf16[4,8,4096]{2,1,0:T(8,128)(2,1)}, bf16[4,8,4096]{2,1,0:T(8,128)(2,1)}, bf16[4,8,4096]{2,1,0:T(8,128)(2,...) custom-call(s32[32]{0:T(128)} %reshape.130.slot_ref, ...), custom_call_target="tpu_custom_call" | custom-call | tf_op jit(solution)/shard_map/pallas_call | solution.py:84
  184.0 2.1 collective-permute-start.26
  186.1 3.8 %collective-permute-done.22.refs_2_ = bf16[4,8,4096]{2,1,0:T(8,128)(2,1)S(1)} collective-permute-done((bf16[4,8,4096]{2,1,0:T(8,128)(2,1)}, bf16[4,8,4096]{2,1,0:T(8,128)(2,1)S(1)}, u32[]{:S(2)}, u32[]{:S(2)}) %collective-permute-start.22) | collective-permute-done | bytes 262176 | tf_op jit(solution)/shard_map/ppermute | solution.py:170
  189.9 2.6 collective-permute-start.27
  192.6 9.7 %collective-permute-done.23.refs_3_ = bf16[4,8,4096]{2,1,0:T(8,128)(2,1)S(1)} collective-permute-done((bf16[4,8,4096]{2,1,0:T(8,128)(2,1)}, bf16[4,8,4096]{2,1,0:T(8,128)(2,1)S(1)}, u32[]{:S(2)}, u32[]{:S(2)}) %collective-permute-start.23) | collective-permute-done | bytes 262176 | tf_op jit(solution)/shard_map/ppermute | solution.py:170
  203.2 2.6 collective-permute-done.25.refs_5_
  205.8 11.1 %collective-permute-start.12 = (bf16[4,8,4096]{2,1,0:T(8,128)(2,1)}, bf16[4,8,4096]{2,1,0:T(8,128)(2,1)S(1)}, u32[]{:S(2)}, u32[]{:S(2)}) collective-permute-start(bf16[4,8,4096]{2,1,0:T(8,128)(2,1)} %get-tuple-element.55), channel_id=1, source_target_pairs={{0,24},{4,28},{8,16},{12,20},{16,8},{20,12},{24,0},{28,4},{1,25},{... | collective-permute-start | bytes 786440 | tf_op jit(solution)/shard_map/ppermute | solution.py:170
  217.0 1.4 collective-permute-done.27.refs_7_
  218.4 15.9 %collective-permute-done.10.refs_4_ = bf16[4,8,4096]{2,1,0:T(8,128)(2,1)S(1)} collective-permute-done((bf16[4,8,4096]{2,1,0:T(8,128)(2,1)}, bf16[4,8,4096]{2,1,0:T(8,128)(2,1)S(1)}, u32[]{:S(2)}, u32[]{:S(2)}) %collective-permute-start.10) | collective-permute-done | bytes 262176 | tf_op jit(solution)/shard_map/ppermute | solution.py:170
  234.3 1.1 collective-permute-start.8
  235.5 4.4 %shard_map.82 = (bf16[4,8,4096]{2,1,0:T(8,128)(2,1)}, bf16[4,8,4096]{2,1,0:T(8,128)(2,1)}, bf16[4,8,4096]{2,1,0:T(8,128)(2,1)}, bf16[4,8,4096]{2,1,0:T(8,128)(2,...) custom-call(s32[32]{0:T(128)} %reshape.130.slot_ref, ...), custom_call_target="tpu_custom_call" | custom-call | tf_op jit(solution)/shard_map/pallas_call | solution.py:84
  240.0 1.3 collective-permute-start.9
  242.1 1.3 collective-permute-start.16
  243.8 5.0 %all-to-all-start.4 = ((f32[32,8,128]{2,1,0:T(8,128)}), f32[32,8,128]{2,1,0:T(8,128)S(1)}, u32[]{:S(2)}, u32[]{:S(2)}) async-start(f32[32,8,128]{2,1,0:T(8,128)} %bitcast.12), calls=%async_computation.4 | async-start | bytes 262144 | tf_op jit(solution)/shard_map/all_to_all | solution.py:175
  248.8 4.5 %shard_map.80 = (bf16[4,8,4096]{2,1,0:T(8,128)(2,1)}, bf16[4,8,4096]{2,1,0:T(8,128)(2,1)}, bf16[4,8,4096]{2,1,0:T(8,128)(2,1)}, bf16[4,8,4096]{2,1,0:T(8,128)(2,...) custom-call(s32[32]{0:T(128)} %reshape.130.slot_ref, ...), custom_call_target="tpu_custom_call" | custom-call | tf_op jit(solution)/shard_map/pallas_call | solution.py:84
  253.4 1.5 collective-permute-start.18
  254.9 1.2 collective-permute-start.19
  256.1 1.5 collective-permute-start.20
  257.5 3.9 %collective-permute-done.16.refs_3_ = bf16[4,8,4096]{2,1,0:T(8,128)(2,1)} collective-permute-done((bf16[4,8,4096]{2,1,0:T(8,128)(2,1)}, bf16[4,8,4096]{2,1,0:T(8,128)(2,1)}, u32[]{:S(2)}, u32[]{:S(2)}) %collective-permute-start.16) | collective-permute-done | bytes 262176 | tf_op jit(solution)/shard_map/ppermute | solution.py:170
  262.5 11.1 %collective-permute-done.18.refs_5_ = bf16[4,8,4096]{2,1,0:T(8,128)(2,1)S(1)} collective-permute-done((bf16[4,8,4096]{2,1,0:T(8,128)(2,1)}, bf16[4,8,4096]{2,1,0:T(8,128)(2,1)S(1)}, u32[]{:S(2)}, u32[]{:S(2)}) %collective-permute-start.18) | collective-permute-done | bytes 262176 | tf_op jit(solution)/shard_map/ppermute | solution.py:170
  273.7 1.2 collective-permute-start.2
  274.8 1.2 collective-permute-start.3
  276.9 1.2 collective-permute-start.5
  278.5 1.7 collective-permute-start.6
  280.7 4.4 %shard_map.85.refs_8_ = bf16[4,32,32768]{2,1,0:T(8,128)(2,1)} custom-call(s32[8]{0:T(128)} %iota_xor_fusion.place_ref, bf16[4,8,4096]{2,1,0:T(8,128)(2,1)} %get-tuple-element.65.refs_0_, bf16[4,8,4096]{2,1,0:T(8,128)(2,1)} %copy-done.19, bf16[4,8,4096]{2,1,0:T(8,128)(2,1)} %copy-done.20, bf16[4,8,4096]{2,1,0:T(8,128)(2,1)} %copy-done.21, ...), custom_call_target="tpu_custom_call" | custom-call | tf_op jit(solution)/shard_map/pallas_call | solution.py:107
  286.6 4.4 %shard_map.86.refs_8_ = bf16[4,32,32768]{2,1,0:T(8,128)(2,1)} custom-call(s32[8]{0:T(128)} %iota_xor_fusion.place_ref, bf16[4,8,4096]{2,1,0:T(8,128)(2,1)} %get-tuple-element.57.refs_0_, bf16[4,8,4096]{2,1,0:T(8,128)(2,1)} %collective-permute-done.14.refs_1_, bf16[4,8,4096]{2,1,0:T(8,128)(2,1)} %collective-permute-done.15.refs_2_, ...), custom_call_target="tpu_custom_call", output_to_operand_aliasing={{}: (9, {})} | custom-call | tf_op jit(solution)/shard_map/pallas_call | solution.py:107
  291.0 4.4 %shard_map.87.refs_8_ = bf16[4,32,32768]{2,1,0:T(8,128)(2,1)} custom-call(s32[8]{0:T(128)} %iota_xor_fusion.place_ref, bf16[4,8,4096]{2,1,0:T(8,128)(2,1)} %get-tuple-element.49.refs_0_, bf16[4,8,4096]{2,1,0:T(8,128)(2,1)} %copy-done.7, bf16[4,8,4096]{2,1,0:T(8,128)(2,1)} %collective-permute-done.8.refs_2_, ...), custom_call_target="tpu_custom_call", output_to_operand_aliasing={{}: (9, {})} | custom-call | tf_op jit(solution)/shard_map/pallas_call | solution.py:107
  295.5 4.4 %collective-permute-done.4.refs_5_ = bf16[4,8,4096]{2,1,0:T(8,128)(2,1)S(1)} collective-permute-done((bf16[4,8,4096]{2,1,0:T(8,128)(2,1)}, bf16[4,8,4096]{2,1,0:T(8,128)(2,1)S(1)}, u32[]{:S(2)}, u32[]{:S(2)}) %collective-permute-start.4) | collective-permute-done | bytes 262176 | tf_op jit(solution)/shard_map/ppermute | solution.py:170
  300.8 4.4 %shard_map.88 = bf16[4,32,32768]{2,1,0:T(8,128)(2,1)} custom-call(s32[8]{0:T(128)} %iota_xor_fusion.place_ref, bf16[4,8,4096]{2,1,0:T(8,128)(2,1)} %get-tuple-element.40.refs_0_, bf16[4,8,4096]{2,1,0:T(8,128)(2,1)} %copy-done.9, bf16[4,8,4096]{2,1,0:T(8,128)(2,1)} %copy-done.10, bf16[4,8,4096]{2,1,0:T(8,128)(2,1)} %copy-done.12, ...), custom_call_target="tpu_custom_call", output_to_operand_aliasing={{}: (9, {})} | custom-call | tf_op jit(solution)/shard_map/pallas_call | solution.py:107
  (131 shorter events, 12.7 us)
Async XLA Ops:
  5.3 54.0 %all-to-all-start.3 = ((bf16[32,8,4096]{2,1,0:T(8,128)(2,1)}), bf16[32,8,4096]{2,1,0:T(8,128)(2,1)S(1)}, u32[]{:S(2)}, u32[]{:S(2)}) async-start(bf16[32,8,4096]{2,1,0:T(8,128)(2,1)} %bitcast.36), calls=%async_computation.3 | async-start | bytes 4194304 | tf_op jit(solution)/shard_map/all_to_all | solution.py:157
  60.7 53.0 %all-to-all-start = ((bf16[32,8,4224]{2,1,0:T(8,128)(2,1)}), bf16[32,8,4224]{2,1,0:T(8,128)(2,1)S(1)}, u32[]{:S(2)}, u32[]{:S(2)}) async-start(bf16[32,8,4224]{2,1,0:T(8,128)(2,1)} %pad_maximum_fusion), calls=%async_computation | async-start | bytes 4325376 | tf_op jit(solution)/shard_map/all_to_all | solution.py:157
  113.7 20.2 %copy-start = (bf16[32,8,4224]{2,1,0:T(8,128)(2,1)}, bf16[32,8,4224]{2,1,0:T(8,128)(2,1)S(1)}, u32[]{:S(2)}) copy-start(bf16[32,8,4224]{2,1,0:T(8,128)(2,1)S(1)} %all-to-all-done.refs_0_.refs_1_.refs_2_.refs_3_.refs_4_.refs_5_.refs_6_.refs_7_) | copy-start | bytes 6488068
  113.7 51.2 %all-to-all-start.2 = ((bf16[32,8,4096]{2,1,0:T(8,128)(2,1)}), bf16[32,8,4096]{2,1,0:T(8,128)(2,1)}, u32[]{:S(2)}, u32[]{:S(2)}) async-start(bf16[32,8,4096]{2,1,0:T(8,128)(2,1)} %bitcast.37), calls=%async_computation.2 | async-start | bytes 4194304 | tf_op jit(solution)/shard_map/all_to_all | solution.py:157
  151.9 17.1 %copy-start.30 = (s32[32]{0:T(128)S(1)}, s32[32]{0:T(128)}, u32[]{:S(2)}) copy-start(s32[32]{0:T(128)} %param.9) | copy-start | bytes 388
  151.9 17.2 %copy-start.28 = (s32[32]{0:T(128)S(1)}, s32[32]{0:T(128)}, u32[]{:S(2)}) copy-start(s32[32]{0:T(128)} %plan_ref.7) | copy-start | bytes 388
  164.9 78.9 %all-to-all-start.1 = ((bf16[32,8,4096]{2,1,0:T(8,128)(2,1)}), bf16[32,8,4096]{2,1,0:T(8,128)(2,1)S(1)}, u32[]{:S(2)}, u32[]{:S(2)}) async-start(bf16[32,8,4096]{2,1,0:T(8,128)(2,1)} %bitcast.35), calls=%async_computation.1 | async-start | bytes 4194304 | tf_op jit(solution)/shard_map/all_to_all | solution.py:157
  175.6 8.3 %collective-permute-start.21 = (bf16[4,8,4096]{2,1,0:T(8,128)(2,1)}, bf16[4,8,4096]{2,1,0:T(8,128)(2,1)S(1)}, u32[]{:S(2)}, u32[]{:S(2)}) collective-permute-start(bf16[4,8,4096]{2,1,0:T(8,128)(2,1)} %get-tuple-element.66), channel_id=1, source_target_pairs={{0,4},{4,0},{8,12},{12,8},{16,20},{20,16},{24,28},{28,24},{1,5},{5... | collective-permute-start | bytes 786440 | tf_op jit(solution)/shard_map/ppermute | solution.py:170
  176.1 13.8 %collective-permute-start.22 = (bf16[4,8,4096]{2,1,0:T(8,128)(2,1)}, bf16[4,8,4096]{2,1,0:T(8,128)(2,1)S(1)}, u32[]{:S(2)}, u32[]{:S(2)}) collective-permute-start(bf16[4,8,4096]{2,1,0:T(8,128)(2,1)} %get-tuple-element.67), channel_id=1, source_target_pairs={{0,8},{4,12},{8,0},{12,4},{16,24},{20,28},{24,16},{28,20},{1,9},{5... | collective-permute-start | bytes 786440 | tf_op jit(solution)/shard_map/ppermute | solution.py:170
  177.3 25.0 %collective-permute-start.23 = (bf16[4,8,4096]{2,1,0:T(8,128)(2,1)}, bf16[4,8,4096]{2,1,0:T(8,128)(2,1)S(1)}, u32[]{:S(2)}, u32[]{:S(2)}) collective-permute-start(bf16[4,8,4096]{2,1,0:T(8,128)(2,1)} %get-tuple-element.68), channel_id=1, source_target_pairs={{0,12},{4,8},{8,4},{12,0},{16,28},{20,24},{24,20},{28,16},{1,13},{... | collective-permute-start | bytes 786440 | tf_op jit(solution)/shard_map/ppermute | solution.py:170
  177.8 25.2 %collective-permute-start.24 = (bf16[4,8,4096]{2,1,0:T(8,128)(2,1)}, bf16[4,8,4096]{2,1,0:T(8,128)(2,1)S(1)}, u32[]{:S(2)}, u32[]{:S(2)}) collective-permute-start(bf16[4,8,4096]{2,1,0:T(8,128)(2,1)} %get-tuple-element.69), channel_id=1, source_target_pairs={{0,16},{4,20},{8,24},{12,28},{16,0},{20,4},{24,8},{28,12},{1,17},{... | collective-permute-start | bytes 786440 | tf_op jit(solution)/shard_map/ppermute | solution.py:170
  179.0 26.8 %collective-permute-start.25 = (bf16[4,8,4096]{2,1,0:T(8,128)(2,1)}, bf16[4,8,4096]{2,1,0:T(8,128)(2,1)S(1)}, u32[]{:S(2)}, u32[]{:S(2)}) collective-permute-start(bf16[4,8,4096]{2,1,0:T(8,128)(2,1)} %get-tuple-element.70), channel_id=1, source_target_pairs={{0,20},{4,16},{8,28},{12,24},{16,4},{20,0},{24,12},{28,8},{1,21},{... | collective-permute-start | bytes 786440 | tf_op jit(solution)/shard_map/ppermute | solution.py:170
  184.0 18.3 %copy-start.19 = (bf16[4,8,4096]{2,1,0:T(8,128)(2,1)}, bf16[4,8,4096]{2,1,0:T(8,128)(2,1)S(1)}, u32[]{:S(2)}) copy-start(bf16[4,8,4096]{2,1,0:T(8,128)(2,1)S(1)} %collective-permute-done.21.refs_1_) | copy-start | bytes 786436
  184.0 32.9 %collective-permute-start.26 = (bf16[4,8,4096]{2,1,0:T(8,128)(2,1)}, bf16[4,8,4096]{2,1,0:T(8,128)(2,1)S(1)}, u32[]{:S(2)}, u32[]{:S(2)}) collective-permute-start(bf16[4,8,4096]{2,1,0:T(8,128)(2,1)} %get-tuple-element.71), channel_id=1, source_target_pairs={{0,24},{4,28},{8,16},{12,20},{16,8},{20,12},{24,0},{28,4},{1,25},{... | collective-permute-start | bytes 786440 | tf_op jit(solution)/shard_map/ppermute | solution.py:170
  189.9 12.3 %copy-start.20 = (bf16[4,8,4096]{2,1,0:T(8,128)(2,1)}, bf16[4,8,4096]{2,1,0:T(8,128)(2,1)S(1)}, u32[]{:S(2)}) copy-start(bf16[4,8,4096]{2,1,0:T(8,128)(2,1)S(1)} %collective-permute-done.22.refs_2_) | copy-start | bytes 786436
  189.9 28.5 %collective-permute-start.27 = (bf16[4,8,4096]{2,1,0:T(8,128)(2,1)}, bf16[4,8,4096]{2,1,0:T(8,128)(2,1)S(1)}, u32[]{:S(2)}, u32[]{:S(2)}) collective-permute-start(bf16[4,8,4096]{2,1,0:T(8,128)(2,1)} %get-tuple-element.72), channel_id=1, source_target_pairs={{0,28},{4,24},{8,20},{12,16},{16,12},{20,8},{24,4},{28,0},{1,29},{... | collective-permute-start | bytes 786440 | tf_op jit(solution)/shard_map/ppermute | solution.py:170
  202.3 32.1 %collective-permute-start.10 = (bf16[4,8,4096]{2,1,0:T(8,128)(2,1)}, bf16[4,8,4096]{2,1,0:T(8,128)(2,1)S(1)}, u32[]{:S(2)}, u32[]{:S(2)}) collective-permute-start(bf16[4,8,4096]{2,1,0:T(8,128)(2,1)} %get-tuple-element.53), channel_id=1, source_target_pairs={{0,16},{4,20},{8,24},{12,28},{16,0},{20,4},{24,8},{28,12},{1,17},{... | collective-permute-start | bytes 786440 | tf_op jit(solution)/shard_map/ppermute | solution.py:170
  203.1 37.0 %collective-permute-start.11 = (bf16[4,8,4096]{2,1,0:T(8,128)(2,1)}, bf16[4,8,4096]{2,1,0:T(8,128)(2,1)S(1)}, u32[]{:S(2)}, u32[]{:S(2)}) collective-permute-start(bf16[4,8,4096]{2,1,0:T(8,128)(2,1)} %get-tuple-element.54), channel_id=1, source_target_pairs={{0,20},{4,16},{8,28},{12,24},{16,4},{20,0},{24,12},{28,8},{1,21},{... | collective-permute-start | bytes 786440 | tf_op jit(solution)/shard_map/ppermute | solution.py:170
  205.8 11.1 %copy-start.23 = (bf16[4,8,4096]{2,1,0:T(8,128)(2,1)}, bf16[4,8,4096]{2,1,0:T(8,128)(2,1)S(1)}, u32[]{:S(2)}) copy-start(bf16[4,8,4096]{2,1,0:T(8,128)(2,1)S(1)} %collective-permute-done.25.refs_5_) | copy-start | bytes 786436
  205.8 35.5 %collective-permute-start.12 = (bf16[4,8,4096]{2,1,0:T(8,128)(2,1)}, bf16[4,8,4096]{2,1,0:T(8,128)(2,1)S(1)}, u32[]{:S(2)}, u32[]{:S(2)}) collective-permute-start(bf16[4,8,4096]{2,1,0:T(8,128)(2,1)} %get-tuple-element.55), channel_id=1, source_target_pairs={{0,24},{4,28},{8,16},{12,20},{16,8},{20,12},{24,0},{28,4},{1,25},{... | collective-permute-start | bytes 786440 | tf_op jit(solution)/shard_map/ppermute | solution.py:170
  216.9 17.4 %copy-start.24 = (bf16[4,8,4096]{2,1,0:T(8,128)(2,1)}, bf16[4,8,4096]{2,1,0:T(8,128)(2,1)S(1)}, u32[]{:S(2)}) copy-start(bf16[4,8,4096]{2,1,0:T(8,128)(2,1)S(1)} %collective-permute-done.26.refs_6_) | copy-start | bytes 786436
  216.9 24.6 %collective-permute-start.13 = (bf16[4,8,4096]{2,1,0:T(8,128)(2,1)}, bf16[4,8,4096]{2,1,0:T(8,128)(2,1)S(1)}, u32[]{:S(2)}, u32[]{:S(2)}) collective-permute-start(bf16[4,8,4096]{2,1,0:T(8,128)(2,1)} %get-tuple-element.56), channel_id=1, source_target_pairs={{0,28},{4,24},{8,20},{12,16},{16,12},{20,8},{24,4},{28,0},{1,29},{... | collective-permute-start | bytes 786440 | tf_op jit(solution)/shard_map/ppermute | solution.py:170
  218.4 15.9 %copy-start.25 = (bf16[4,8,4096]{2,1,0:T(8,128)(2,1)}, bf16[4,8,4096]{2,1,0:T(8,128)(2,1)S(1)}, u32[]{:S(2)}) copy-start(bf16[4,8,4096]{2,1,0:T(8,128)(2,1)S(1)} %collective-permute-done.27.refs_7_) | copy-start | bytes 786436
  218.4 23.7 %collective-permute-start.7 = (bf16[4,8,4096]{2,1,0:T(8,128)(2,1)}, bf16[4,8,4096]{2,1,0:T(8,128)(2,1)S(1)}, u32[]{:S(2)}, u32[]{:S(2)}) collective-permute-start(bf16[4,8,4096]{2,1,0:T(8,128)(2,1)} %get-tuple-element.50), channel_id=1, source_target_pairs={{0,4},{4,0},{8,12},{12,8},{16,20},{20,16},{24,28},{28,24},{1,5},{5... | collective-permute-start | bytes 786440 | tf_op jit(solution)/shard_map/ppermute | solution.py:170
  234.3 9.1 %collective-permute-start.8 = (bf16[4,8,4096]{2,1,0:T(8,128)(2,1)}, bf16[4,8,4096]{2,1,0:T(8,128)(2,1)}, u32[]{:S(2)}, u32[]{:S(2)}) collective-permute-start(bf16[4,8,4096]{2,1,0:T(8,128)(2,1)} %get-tuple-element.51), channel_id=1, source_target_pairs={{0,8},{4,12},{8,0},{12,4},{16,24},{20,28},{24,16},{28,20},{1,9},{5... | collective-permute-start | bytes 786440 | tf_op jit(solution)/shard_map/ppermute | solution.py:170
  240.0 13.3 %copy-start.4 = (bf16[4,8,4096]{2,1,0:T(8,128)(2,1)}, bf16[4,8,4096]{2,1,0:T(8,128)(2,1)S(1)}, u32[]{:S(2)}) copy-start(bf16[4,8,4096]{2,1,0:T(8,128)(2,1)S(1)} %collective-permute-done.11.refs_5_) | copy-start | bytes 786436
  240.0 13.3 %collective-permute-start.9 = (bf16[4,8,4096]{2,1,0:T(8,128)(2,1)}, bf16[4,8,4096]{2,1,0:T(8,128)(2,1)S(1)}, u32[]{:S(2)}, u32[]{:S(2)}) collective-permute-start(bf16[4,8,4096]{2,1,0:T(8,128)(2,1)} %get-tuple-element.52), channel_id=1, source_target_pairs={{0,12},{4,8},{8,4},{12,0},{16,28},{20,24},{24,20},{28,16},{1,13},{... | collective-permute-start | bytes 786440 | tf_op jit(solution)/shard_map/ppermute | solution.py:170
  241.3 12.0 %copy-start.5 = (bf16[4,8,4096]{2,1,0:T(8,128)(2,1)}, bf16[4,8,4096]{2,1,0:T(8,128)(2,1)S(1)}, u32[]{:S(2)}) copy-start(bf16[4,8,4096]{2,1,0:T(8,128)(2,1)S(1)} %collective-permute-done.12.refs_6_) | copy-start | bytes 786436
  241.3 13.6 %collective-permute-start.14 = (bf16[4,8,4096]{2,1,0:T(8,128)(2,1)}, bf16[4,8,4096]{2,1,0:T(8,128)(2,1)}, u32[]{:S(2)}, u32[]{:S(2)}) collective-permute-start(bf16[4,8,4096]{2,1,0:T(8,128)(2,1)} %get-tuple-element.58), channel_id=1, source_target_pairs={{0,4},{4,0},{8,12},{12,8},{16,20},{20,16},{24,28},{28,24},{1,5},{5... | collective-permute-start | bytes 786440 | tf_op jit(solution)/shard_map/ppermute | solution.py:170
  241.5 11.8 %copy-start.6 = (bf16[4,8,4096]{2,1,0:T(8,128)(2,1)}, bf16[4,8,4096]{2,1,0:T(8,128)(2,1)S(1)}, u32[]{:S(2)}) copy-start(bf16[4,8,4096]{2,1,0:T(8,128)(2,1)S(1)} %collective-permute-done.13.refs_7_) | copy-start | bytes 786436
  241.5 14.5 %collective-permute-start.15 = (bf16[4,8,4096]{2,1,0:T(8,128)(2,1)}, bf16[4,8,4096]{2,1,0:T(8,128)(2,1)}, u32[]{:S(2)}, u32[]{:S(2)}) collective-permute-start(bf16[4,8,4096]{2,1,0:T(8,128)(2,1)} %get-tuple-element.59), channel_id=1, source_target_pairs={{0,8},{4,12},{8,0},{12,4},{16,24},{20,28},{24,16},{28,20},{1,9},{5... | collective-permute-start | bytes 786440 | tf_op jit(solution)/shard_map/ppermute | solution.py:170
  242.1 11.2 %copy-start.7 = (bf16[4,8,4096]{2,1,0:T(8,128)(2,1)}, bf16[4,8,4096]{2,1,0:T(8,128)(2,1)S(1)}, u32[]{:S(2)}) copy-start(bf16[4,8,4096]{2,1,0:T(8,128)(2,1)S(1)} %collective-permute-done.7.refs_1_) | copy-start | bytes 786436
  242.1 19.3 %collective-permute-start.16 = (bf16[4,8,4096]{2,1,0:T(8,128)(2,1)}, bf16[4,8,4096]{2,1,0:T(8,128)(2,1)}, u32[]{:S(2)}, u32[]{:S(2)}) collective-permute-start(bf16[4,8,4096]{2,1,0:T(8,128)(2,1)} %get-tuple-element.60), channel_id=1, source_target_pairs={{0,12},{4,8},{8,4},{12,0},{16,28},{20,24},{24,20},{28,16},{1,13},{... | collective-permute-start | bytes 786440 | tf_op jit(solution)/shard_map/ppermute | solution.py:170
  243.5 18.4 %collective-permute-start.17 = (bf16[4,8,4096]{2,1,0:T(8,128)(2,1)}, bf16[4,8,4096]{2,1,0:T(8,128)(2,1)}, u32[]{:S(2)}, u32[]{:S(2)}) collective-permute-start(bf16[4,8,4096]{2,1,0:T(8,128)(2,1)} %get-tuple-element.61), channel_id=1, source_target_pairs={{0,16},{4,20},{8,24},{12,28},{16,0},{20,4},{24,8},{28,12},{1,17},{... | collective-permute-start | bytes 786440 | tf_op jit(solution)/shard_map/ppermute | solution.py:170
  243.8 41.4 %all-to-all-start.4 = ((f32[32,8,128]{2,1,0:T(8,128)}), f32[32,8,128]{2,1,0:T(8,128)S(1)}, u32[]{:S(2)}, u32[]{:S(2)}) async-start(f32[32,8,128]{2,1,0:T(8,128)} %bitcast.12), calls=%async_computation.4 | async-start | bytes 262144 | tf_op jit(solution)/shard_map/all_to_all | solution.py:175
  253.4 31.8 %copy-start.8 = (bf16[4,8,4096]{2,1,0:T(8,128)(2,1)}, bf16[4,8,4096]{2,1,0:T(8,128)(2,1)S(1)}, u32[]{:S(2)}) copy-start(bf16[4,8,4096]{2,1,0:T(8,128)(2,1)S(1)} %collective-permute-done.9.refs_3_) | copy-start | bytes 786436
  253.4 20.3 %collective-permute-start.18 = (bf16[4,8,4096]{2,1,0:T(8,128)(2,1)}, bf16[4,8,4096]{2,1,0:T(8,128)(2,1)S(1)}, u32[]{:S(2)}, u32[]{:S(2)}) collective-permute-start(bf16[4,8,4096]{2,1,0:T(8,128)(2,1)} %get-tuple-element.62), channel_id=1, source_target_pairs={{0,20},{4,16},{8,28},{12,24},{16,4},{20,0},{24,12},{28,8},{1,21},{... | collective-permute-start | bytes 786440 | tf_op jit(solution)/shard_map/ppermute | solution.py:170
  254.9 19.9 %collective-permute-start.19 = (bf16[4,8,4096]{2,1,0:T(8,128)(2,1)}, bf16[4,8,4096]{2,1,0:T(8,128)(2,1)S(1)}, u32[]{:S(2)}, u32[]{:S(2)}) collective-permute-start(bf16[4,8,4096]{2,1,0:T(8,128)(2,1)} %get-tuple-element.63), channel_id=1, source_target_pairs={{0,24},{4,28},{8,16},{12,20},{16,8},{20,12},{24,0},{28,4},{1,25},{... | collective-permute-start | bytes 786440 | tf_op jit(solution)/shard_map/ppermute | solution.py:170
  256.1 19.9 %collective-permute-start.20 = (bf16[4,8,4096]{2,1,0:T(8,128)(2,1)}, bf16[4,8,4096]{2,1,0:T(8,128)(2,1)S(1)}, u32[]{:S(2)}, u32[]{:S(2)}) collective-permute-start(bf16[4,8,4096]{2,1,0:T(8,128)(2,1)} %get-tuple-element.64), channel_id=1, source_target_pairs={{0,28},{4,24},{8,20},{12,16},{16,12},{20,8},{24,4},{28,0},{1,29},{... | collective-permute-start | bytes 786440 | tf_op jit(solution)/shard_map/ppermute | solution.py:170
  261.4 15.4 %collective-permute-start = (bf16[4,8,4096]{2,1,0:T(8,128)(2,1)}, bf16[4,8,4096]{2,1,0:T(8,128)(2,1)S(1)}, u32[]{:S(2)}, u32[]{:S(2)}) collective-permute-start(bf16[4,8,4096]{2,1,0:T(8,128)(2,1)} %get-tuple-element.41), channel_id=1, source_target_pairs={{0,4},{4,0},{8,12},{12,8},{16,20},{20,16},{24,28},{28,24},{1,5},{5... | collective-permute-start | bytes 786440 | tf_op jit(solution)/shard_map/ppermute | solution.py:170
  261.8 16.7 %collective-permute-start.1 = (bf16[4,8,4096]{2,1,0:T(8,128)(2,1)}, bf16[4,8,4096]{2,1,0:T(8,128)(2,1)S(1)}, u32[]{:S(2)}, u32[]{:S(2)}) collective-permute-start(bf16[4,8,4096]{2,1,0:T(8,128)(2,1)} %get-tuple-element.42), channel_id=1, source_target_pairs={{0,8},{4,12},{8,0},{12,4},{16,24},{20,28},{24,16},{28,20},{1,9},{5... | collective-permute-start | bytes 786440 | tf_op jit(solution)/shard_map/ppermute | solution.py:170
  273.7 11.5 %copy-start.11 = (bf16[4,8,4096]{2,1,0:T(8,128)(2,1)}, bf16[4,8,4096]{2,1,0:T(8,128)(2,1)S(1)}, u32[]{:S(2)}) copy-start(bf16[4,8,4096]{2,1,0:T(8,128)(2,1)S(1)} %collective-permute-done.18.refs_5_) | copy-start | bytes 786436
  273.7 21.8 %collective-permute-start.2 = (bf16[4,8,4096]{2,1,0:T(8,128)(2,1)}, bf16[4,8,4096]{2,1,0:T(8,128)(2,1)S(1)}, u32[]{:S(2)}, u32[]{:S(2)}) collective-permute-start(bf16[4,8,4096]{2,1,0:T(8,128)(2,1)} %get-tuple-element.43), channel_id=1, source_target_pairs={{0,12},{4,8},{8,4},{12,0},{16,28},{20,24},{24,20},{28,16},{1,13},{... | collective-permute-start | bytes 786440 | tf_op jit(solution)/shard_map/ppermute | solution.py:170
  274.8 10.4 %copy-start.13 = (bf16[4,8,4096]{2,1,0:T(8,128)(2,1)}, bf16[4,8,4096]{2,1,0:T(8,128)(2,1)S(1)}, u32[]{:S(2)}) copy-start(bf16[4,8,4096]{2,1,0:T(8,128)(2,1)S(1)} %collective-permute-done.19.refs_6_) | copy-start | bytes 786436
  274.8 20.7 %collective-permute-start.3 = (bf16[4,8,4096]{2,1,0:T(8,128)(2,1)}, bf16[4,8,4096]{2,1,0:T(8,128)(2,1)S(1)}, u32[]{:S(2)}, u32[]{:S(2)}) collective-permute-start(bf16[4,8,4096]{2,1,0:T(8,128)(2,1)} %get-tuple-element.44), channel_id=1, source_target_pairs={{0,16},{4,20},{8,24},{12,28},{16,0},{20,4},{24,8},{28,12},{1,17},{... | collective-permute-start | bytes 786440 | tf_op jit(solution)/shard_map/ppermute | solution.py:170
  276.0 23.9 %collective-permute-start.4 = (bf16[4,8,4096]{2,1,0:T(8,128)(2,1)}, bf16[4,8,4096]{2,1,0:T(8,128)(2,1)S(1)}, u32[]{:S(2)}, u32[]{:S(2)}) collective-permute-start(bf16[4,8,4096]{2,1,0:T(8,128)(2,1)} %get-tuple-element.45), channel_id=1, source_target_pairs={{0,20},{4,16},{8,28},{12,24},{16,4},{20,0},{24,12},{28,8},{1,21},{... | collective-permute-start | bytes 786440 | tf_op jit(solution)/shard_map/ppermute | solution.py:170
  276.9 23.0 %collective-permute-start.5 = (bf16[4,8,4096]{2,1,0:T(8,128)(2,1)}, bf16[4,8,4096]{2,1,0:T(8,128)(2,1)S(1)}, u32[]{:S(2)}, u32[]{:S(2)}) collective-permute-start(bf16[4,8,4096]{2,1,0:T(8,128)(2,1)} %get-tuple-element.46), channel_id=1, source_target_pairs={{0,24},{4,28},{8,16},{12,20},{16,8},{20,12},{24,0},{28,4},{1,25},{... | collective-permute-start | bytes 786440 | tf_op jit(solution)/shard_map/ppermute | solution.py:170
  278.5 21.4 %collective-permute-start.6 = (bf16[4,8,4096]{2,1,0:T(8,128)(2,1)}, bf16[4,8,4096]{2,1,0:T(8,128)(2,1)S(1)}, u32[]{:S(2)}, u32[]{:S(2)}) collective-permute-start(bf16[4,8,4096]{2,1,0:T(8,128)(2,1)} %get-tuple-element.47), channel_id=1, source_target_pairs={{0,28},{4,24},{8,20},{12,16},{16,12},{20,8},{24,4},{28,0},{1,29},{... | collective-permute-start | bytes 786440 | tf_op jit(solution)/shard_map/ppermute | solution.py:170
  (16 other events, 65.8 us)
